TPU v7x, 128 devices: a whole 4x4x4 slice. The times are simulated.
128 devices in a mesh: row: 16 (over y, z), col: 8 (over x, core).
Axes of the slice: x: 4, y: 4, z: 4, core: 2. Of those that a mesh axis runs over, the one named last changes fastest.
Arguments:
- matrix_tiles: bfloat16 [16, 8, 96, 256, 256], P('row', 'col'), may hold values from -0.0546875 to 0.0546875
- tile_rows: int32 [16, 8, 96], P('row', 'col'), may hold values from 0 to 7, as said below
- tile_cols: int32 [16, 8, 96], P('row', 'col'), may hold values from 0 to 15
- tile_count: int32 [16, 8], P('row', 'col'), may hold values from 24 to 96, as said below
- x_start: float32 [32768, 256], P(('col', 'row')), may hold values from -5 to 5
- y_start: float32 [32768, 256], P(('row', 'col')), may hold values from 0 to 1
- cost_vector: float32 [32768, 256], P(('col', 'row')), may hold values from -6 to 6
- right_side: float32 [32768, 256], P(('row', 'col')), may hold values from -6 to 6
- lower_bound: float32 [32768, 256], P(('col', 'row')), may hold values from -1.5 to -0.3
- upper_bound: float32 [32768, 256], P(('col', 'row')), may hold values from 0.3 to 1.5
- step_primal: float32 [256], replicated, may hold values from 0.2 to 0.45
- step_dual: float32 [256], replicated, may hold values from 0.2 to 0.45
Outputs:
- primal_out: float32 [32768, 256], P(('col', 'row'))
- dual_out: float32 [32768, 256], P(('row', 'col'))
Inputs may be any that keep to these rules, and one draw needn't show every extreme that they name: Within one grid cell the pairs (tile_rows, tile_cols) of its slots are all different. `tile_count`: some grid cell has 96 used slots in every draw; slots at or above a cell's count are not part of A.
All inputs are finite; a program needn't handle non-finite values.
Results may differ from a plain program's by a relative error of at most 0.001.
Values may be sent and summed in bfloat16 or wider, within the bound.
No kernel may reach another device: no remote copies, remote signals or barrier semaphores. Data moves between devices by JAX's collectives and lax.ppermute only.
A program may use at most 128 MiB of HBM per device.

v0:
```python
import jax
import jax.numpy as jnp
from jax import lax
from jax.experimental import pallas as pl
from jax.experimental.pallas import tpu as pltpu
from jax.sharding import Mesh
from jax.sharding import PartitionSpec as P


ROW = ("row_0", "row_1")
COL = ("col_0", "col_1")
ROW_COL = ("row_0", "row_1", "col_0", "col_1")
COL_ROW = ("col_0", "col_1", "row_0", "row_1")

NR = 8
NC = 16
T = 256
EXTRA = 16
TALL = T + EXTRA
EPS = 1e-06
f32 = jnp.float32
bf16 = jnp.bfloat16

VMEM = pl.BlockSpec(memory_space=pltpu.VMEM)
SMEM = pl.BlockSpec(memory_space=pltpu.SMEM)
MIB = 1 << 20


def three_parts(v):
    high = v.astype(bf16)
    rest = v - high.astype(f32)
    middle = rest.astype(bf16)
    low = (rest - middle.astype(f32)).astype(bf16)
    row = lax.broadcasted_iota(jnp.int32, (EXTRA, T), 0)
    out = jnp.where(row == 0, high.astype(f32), 0.0)
    out = jnp.where(row == 1, middle.astype(f32), out)
    return jnp.where(row == 2, low.astype(f32), out).astype(bf16)


def sum_of_parts(blocks, height=T):
    total = blocks[0][height:, :].astype(f32)
    for block in blocks[1:]:
        total = total + block[height:, :].astype(f32)
    return jnp.sum(total, axis=0, keepdims=True)


def one_row(v):
    row = lax.broadcasted_iota(jnp.int32, (WIDE - T, T), 0)
    return jnp.where(row == 0, v, 0.0)


N4 = 4
WIDE = T + 8
REST = (N4 - 1) * T


def dense_kernel(rows, cols, count, tiles, dense, table):
    at_y, at_z, at_x, core = (lax.axis_index(name) for name in ROW_COL)

    def clear(k, carry):
        table[k] = -1
        return carry

    def note(slot, carry):
        row, col = rows[0, 0, slot], cols[0, 0, slot]
        r = ((row // 2 - at_x) & 3) + jnp.where((row & 1) == core, 0, N4)
        y, z = (col // N4 - at_y) & 3, (col - at_z) & 3
        big, small = jnp.where(core == 0, y, z), jnp.where(core == 0, z, y)
        table[r * NC + big * N4 + small] = slot
        return carry

    def move(k, carry):
        slot = table[k]
        dense[k] = tiles[0, 0, jnp.maximum(slot, 0)] * jnp.where(slot >= 0, 1.0, 0.0).astype(bf16)
        return carry

    lax.fori_loop(0, NR * NC, clear, 0)
    lax.fori_loop(0, count[0, 0], note, 0)
    lax.fori_loop(0, NR * NC, move, 0)


def make_dense(rows, cols, count, tiles):
    return pl.pallas_call(
        dense_kernel,
        out_shape=jax.ShapeDtypeStruct((NR * NC, T, T), bf16),
        in_specs=[SMEM, SMEM, SMEM, VMEM],
        out_specs=VMEM,
        scratch_shapes=[pltpu.SMEM((NR * NC,), jnp.int32)],
        compiler_params=pltpu.CompilerParams(vmem_limit_bytes=4 * MIB),
        name="dense",
    )(rows, cols, count, tiles)


def call(kernel, outs, *args, grant=10):
    return pl.pallas_call(
        kernel,
        out_shape=[jax.ShapeDtypeStruct(shape, kind) for shape, kind in outs],
        in_specs=[VMEM] * len(args),
        out_specs=[VMEM] * len(outs),
        compiler_params=pltpu.CompilerParams(vmem_limit_bytes=grant * MIB),
    )(*args)


def multiply(kernel, dense, pieces, outs, tiles):
    return pl.pallas_call(
        kernel,
        out_shape=[jax.ShapeDtypeStruct(*out) for out in outs],
        in_specs=[VMEM] * (1 + len(pieces)),
        out_specs=[VMEM] * len(outs),
        cost_estimate=pl.CostEstimate(flops=tiles * 2 * T**3, bytes_accessed=tiles * 2 * T * T, transcendentals=0),
        compiler_params=pltpu.CompilerParams(vmem_limit_bytes=16 * MIB),
    )(dense, *pieces)


def back(k):
    return -k % N4


def forward(dense, near, firsts, rests, far, extra):
    def kernel(dense, *refs):
        near, firsts, rests, out = refs[:N4], refs[N4 : 2 * N4 - 1], refs[2 * N4 - 1 : -1], refs[-1]
        if extra:
            total = sum_of_parts(near) + sum_of_parts(rests, REST)
            out[:, T:, :] = jnp.broadcast_to(one_row(total)[None], (N4, WIDE - T, T))
        first = N4 if far else 0
        places = [back(b) * N4 + back(a) for b in range(N4) for a in range(N4)]
        left = jnp.concatenate(
            [jnp.concatenate([dense[(first + k) * NC + c] for c in places], axis=1) for k in range(N4)], axis=0
        )
        right = [tile[:T, :] for tile in near]
        for one, rest in zip(firsts, rests):
            right += [one[:T, :], rest[:REST, :]]
        product = jnp.dot(left, jnp.concatenate(right, axis=0), preferred_element_type=f32)
        out[:, :T, :] = product.reshape(N4, T, T)

    tall = WIDE if extra else T
    outs = [((N4, tall, T), f32)]
    return multiply(kernel, dense, [*near, *firsts, *rests], outs, N4 * NC)[0]


def transposed_product(dense, pieces, places):
    left = jnp.concatenate([piece[:T, :] for piece in pieces], axis=1)
    rows = [first + back(k) for first in (0, N4) for k in range(N4)]
    right = jnp.concatenate(
        [jnp.concatenate([dense[r * NC + c] for r in rows], axis=0) for c in places], axis=1
    )
    product = jnp.dot(left, right, preferred_element_type=f32)
    return [product[:, k * T : (k + 1) * T] for k in range(len(places))]


def backward_rest(dense, pieces, group, extra):
    def kernel(dense, *refs):
        pieces, out = refs[:-1], refs[-1]
        if extra:
            out[REST:, :] = three_parts(sum_of_parts(pieces))
        for a, block in enumerate(transposed_product(dense, pieces, range(group * N4 + 1, group * N4 + N4))):
            out[a * T : (a + 1) * T, :] = block.astype(bf16)

    outs = [((REST + (EXTRA if extra else 0), T), bf16)]
    return multiply(kernel, dense, pieces, outs, (N4 - 1) * NR)[0]


def backward_near(dense, pieces, extra):
    def kernel(dense, *refs):
        pieces, (own, rest, moved), firsts = refs[: 2 * N4], refs[2 * N4 : 2 * N4 + 3], refs[2 * N4 + 3 :]
        moved[...] = sum_of_parts(pieces) if extra else jnp.zeros((1, T), f32)
        blocks = transposed_product(dense, pieces, [0, 1, 2, 3, 4, 8, 12])
        own[...] = blocks[0]
        for a in range(1, N4):
            rest[(a - 1) * T : a * T, :] = blocks[a]
        for out, block in zip(firsts, blocks[N4:]):
            out[...] = block.astype(bf16)

    outs = [((T, T), f32), ((REST, T), f32), ((1, T), f32)] + [((T, T), bf16)] * (N4 - 1)
    own, rest, moved, *firsts = multiply(kernel, dense, pieces, outs, 7 * NR)
    return own, rest, moved, firsts


def big_sum_kernel(extra, own, own_moved, *refs):
    rests, outs, moved = refs[: N4 - 1], refs[N4 - 1 : -1], refs[-1]
    total = own_moved[...]
    if extra:
        total = total + sum_of_parts(rests, REST)
    moved[...] = total
    for a, out in enumerate(outs):
        block = own[a * T : (a + 1) * T, :]
        for rest in rests:
            block = block + rest[a * T : (a + 1) * T, :].astype(f32)
        out[:T, :] = block
        if extra:
            out[T:, :] = one_row(total)


def join_kernel(extra, mine, other, *outs):
    if extra:
        total = jnp.sum(mine[0, T:, :] + other[0, T:, :], axis=0, keepdims=True)
    for k, out in enumerate(outs):
        out[:T, :] = (mine[k, :T, :] + other[k, :T, :]).astype(out.dtype)
        if extra:
            out[T:, :] = three_parts(total) if k else one_row(total)


def block_sum(refs):
    total = refs[0][:T, :].astype(f32)
    for ref in refs[1:]:
        total = total + ref[:T, :].astype(f32)
    return total


def rest_kernel(extra, *refs):
    near, out = refs[:N4], refs[N4]
    for a in range(1, N4):
        out[(a - 1) * T : a * T, :] = near[a][:T, :]
    if extra:
        out[REST:, :] = three_parts(sum_of_parts(near))


BLOCKS = 2 * N4 - 1


def primal_one_kernel(*refs):
    grads, (x, cost, low, high, step, primal, ahead) = refs[:BLOCKS], refs[BLOCKS:]
    grad = block_sum(grads).T
    one = jnp.clip(x[...] - step[...] * (cost[...] - grad), low[...], high[...])
    primal[...] = one
    diff = one - x[...]
    ahead[:T, :] = (2.0 * one - x[...]).astype(bf16)
    ahead[T:, :] = three_parts(jnp.sum(diff * diff, axis=0, keepdims=True))


def dual_one_kernel(*refs):
    images, (y, side, step, dual, moved, flipped) = refs[:N4], refs[N4:]
    image = block_sum(images)
    moved[...] = sum_of_parts(images[:1]) + sum_of_parts(images[1:])
    one = jnp.maximum(y[...] + step[...] * (side[...] - image), 0.0)
    dual[...] = one
    diff = one - y[...]
    flipped[:T, :] = one.T.astype(bf16)
    flipped[T:, :] = three_parts(jnp.sum(diff * diff, axis=0, keepdims=True))


def primal_two_kernel(rows, cols, *refs):
    grads = refs[:BLOCKS]
    line, moved, one, cost, low, high, step, primal, weight, ahead = refs[BLOCKS:]
    grad = block_sum(grads).T
    move_dual = line[...] + sum_of_parts(grads[N4:])
    w = jnp.sqrt((move_dual / rows + EPS) / (moved[...] / cols + EPS))
    weight[...] = w
    two = jnp.clip(one[...] - step[...] / w * (cost[...] - grad), low[...], high[...])
    primal[...] = two
    ahead[...] = (2.0 * two - one[...]).astype(bf16)


def dual_two_kernel(*refs):
    images, (one, side, step, weight, dual) = refs[:N4], refs[N4:]
    dual[...] = jnp.maximum(one[...] + step[...] * weight[...] * (side[...] - block_sum(images)), 0.0)


def flip_kernel(y, flipped):
    flipped[...] = y[...].T.astype(bf16)


def permute(value, places):
    return lax.ppermute(value, ROW_COL, [(flat(p), flat(q)) for p, q in places])


def flat(place):
    y, z, x, core = place
    return ((y * N4 + z) * N4 + x) * 2 + core


EVERYONE = [(y, z, x, core) for y in range(N4) for z in range(N4) for x in range(N4) for core in range(2)]


def along_y(p, k):
    return ((p[0] + k) % N4, *p[1:])


def along_z(p, k):
    return (p[0], (p[1] + k) % N4, *p[2:])


def to_big(value, k):
    return permute(value, [(p, along_z(p, k) if p[3] else along_y(p, k)) for p in EVERYONE])


def to_small(value, k):
    return permute(value, [(p, along_y(p, k) if p[3] else along_z(p, k)) for p in EVERYONE])


def to_x(value, k):
    return permute(value, [(p, (*p[:2], (p[2] + k) % N4, p[3])) for p in EVERYONE])


def to_other_core(value):
    return permute(value, [(p, (*p[:3], 1 - p[3])) for p in EVERYONE])


FAR_FIRST = (2, 1, 3)


def sent(values, send):
    arrived = {k: send(values[k - 1], k) for k in FAR_FIRST}
    return [arrived[k] for k in range(1, N4)]


def body(
    matrix_tiles,
    tile_rows,
    tile_cols,
    tile_count,
    x_start,
    y_start,
    cost_vector,
    right_side,
    lower_bound,
    upper_bound,
    step_primal,
    step_dual,
):
    dense = make_dense(tile_rows, tile_cols, tile_count, matrix_tiles)
    everyone = lax.axis_size(ROW) * lax.axis_size(COL)
    total_cols = x_start.shape[0] * everyone
    total_rows = y_start.shape[0] * everyone
    step_p, step_d = step_primal[None], step_dual[None]
    square = ((T, T), f32)
    line = ((1, T), f32)

    def to_columns(flipped, extra, ready=None):
        mine = [flipped] + sent([flipped] * 3, to_x)
        if ready is not None:
            mine[0], ready = lax.optimization_barrier((flipped, ready))
        matrix = dense if ready is None else ready
        pieces = mine + [to_other_core(piece) for piece in mine]
        rests = {k: backward_rest(matrix, pieces, k, extra) for k in FAR_FIRST}
        rests = sent([rests[k] for k in range(1, N4)], to_big)
        own, own_rest, moved, firsts = backward_near(matrix, pieces, extra)
        firsts = sent(firsts, to_big)
        tall = WIDE if extra else T
        *blocks, moved = call(
            lambda *refs: big_sum_kernel(extra, *refs), [((tall, T), f32)] * 3 + [line], own_rest, moved, *rests,
        )
        return [own, *firsts, *sent(blocks, to_small)], moved

    def to_rows(ahead, extra):
        near = [ahead] + sent([ahead] * 3, to_small)
        firsts = sent([ahead] * 3, to_big)
        tall = TALL if extra else T
        (rest,) = call(lambda *refs: rest_kernel(extra, *refs), [((REST + tall - T, T), bf16)], *near)
        rests = sent([rest] * 3, to_big)
        other = to_other_core(forward(dense, near, firsts, rests, True, extra))
        mine = forward(dense, near, firsts, rests, False, extra)
        outs = [((WIDE if extra else T, T), f32)] + [((tall, T), bf16)] * (N4 - 1)
        own, *blocks = call(lambda *refs: join_kernel(extra, *refs), outs, mine, other)
        return [own, *sent(blocks, to_x)]

    (flipped,) = call(flip_kernel, [((T, T), bf16)], y_start)
    grads, _ = to_columns(flipped, False, dense)
    one, ahead = call(
        primal_one_kernel,
        [square, ((TALL, T), bf16)],
        *grads, x_start, cost_vector, lower_bound, upper_bound, step_p,
    )
    images = to_rows(ahead, True)
    dual, moved, flipped = call(
        dual_one_kernel,
        [square, line, ((TALL, T), bf16)],
        *images, y_start, right_side, step_d,
    )
    grads, moved_line = to_columns(flipped, True)
    two, weight, ahead = call(
        lambda *refs: primal_two_kernel(float(total_rows), float(total_cols), *refs),
        [square, line, ((T, T), bf16)],
        *grads, moved_line, moved, one, cost_vector, lower_bound, upper_bound, step_p,
    )
    images = to_rows(ahead, False)
    (dual_out,) = call(dual_two_kernel, [square], *images, dual, right_side, step_d, weight)
    return (two, dual_out)


def solution(mesh):
    torus = Mesh(mesh.devices.reshape(4, 4, 4, 2), ("row_0", "row_1", "col_0", "col_1"))
    in_specs = (
        P(ROW, COL, None, None, None),
        P(ROW, COL, None),
        P(ROW, COL, None),
        P(ROW, COL),
        P(COL_ROW, None),
        P(ROW_COL, None),
        P(COL_ROW, None),
        P(ROW_COL, None),
        P(COL_ROW, None),
        P(COL_ROW, None),
        P(),
        P(),
    )
    out_specs = (P(COL_ROW, None), P(ROW_COL, None))
    return jax.shard_map(body, mesh=torus, in_specs=in_specs, out_specs=out_specs, check_vma=False)
```

profile of v0, /device:TPU:1, one launch (start us, length us, event | category | flops | bytes accessed | tf_op | source)
XLA Modules:
  0.0 194.6 jit_solution(15768935751191610814)
XLA Ops:
  1.7 3.4 %collective-permute-start.2 = (bf16[256,256]{1,0:T(8,128)(2,1)S(1)}, bf16[256,256]{1,0:T(8,128)(2,1)S(1)}, u32[]{:S(2)}, u32[]{:S(2)}) collective-permute-start(bf16[256,256]{1,0:T(8,128)(2,1)S(1)} %shard_map.131.refs_0_), channel_id=1, source_target_pairs={{0,6},{1,7},{2,0},{3,1},{4,2},{5,3},{6,4},{7,5},{8,14},{9,15},{10,... | collective-permute-start | bytes 393224 | tf_op jit(solution)/shard_map/ppermute | solution.py:264
  6.8 4.6 %copy-done = bf16[1,1,96,256,256]{4,3,2,1,0:T(8,128)(2,1)S(1)} copy-done((bf16[1,1,96,256,256]{4,3,2,1,0:T(8,128)(2,1)S(1)}, bf16[1,1,96,256,256]{4,3,2,1,0:T(8,128)(2,1)}, u32[]{:S(2)}) %copy-start) | copy-done | bytes 12582936
  12.7 5.0 %dense.1 = bf16[128,256,256]{2,1,0:T(8,128)(2,1)S(1)} custom-call(s32[1,1,96]{2,1,0:T(1,128)S(1)} %copy-done.10, s32[1,1,96]{2,1,0:T(1,128)S(1)} %copy-done.11, s32[1,1]{1,0:T(1,128)S(6)} %copy.14.count, bf16[1,1,96,256,256]{4,3,2,1,0:T(8,128)(2,1)S(1)} %copy-done), custom_call_target="tpu_custom_call" | custom-call | tf_op jit(solution)/shard_map/dense/pallas_call | solution.py:83
  24.9 3.1 %collective-permute-start.11 = (bf16[768,256]{1,0:T(8,128)(2,1)S(1)}, bf16[768,256]{1,0:T(8,128)(2,1)S(1)}, u32[]{:S(2)}, u32[]{:S(2)}) collective-permute-start(bf16[768,256]{1,0:T(8,128)(2,1)S(1)} %shard_map.134), channel_id=1, source_target_pairs={{0,64},{1,17},{2,66},{3,19},{4,68},{5,21},{6,70},{7,23},{8,72},{9,... | collective-permute-start | bytes 1179656 | tf_op jit(solution)/shard_map/ppermute | solution.py:264
  32.7 3.8 %collective-permute-done.11.refs_3_ = bf16[768,256]{1,0:T(8,128)(2,1)S(1)} collective-permute-done((bf16[768,256]{1,0:T(8,128)(2,1)S(1)}, bf16[768,256]{1,0:T(8,128)(2,1)S(1)}, u32[]{:S(2)}, u32[]{:S(2)}) %collective-permute-start.11) | collective-permute-done | bytes 393248 | tf_op jit(solution)/shard_map/ppermute | solution.py:264
  39.3 2.6 %collective-permute-start.14 = (f32[256,256]{1,0:T(8,128)S(1)}, f32[256,256]{1,0:T(8,128)S(1)}, u32[]{:S(2)}, u32[]{:S(2)}) collective-permute-start(f32[256,256]{1,0:T(8,128)S(1)} %get-tuple-element.48), channel_id=1, source_target_pairs={{0,16},{1,65},{2,18},{3,67},{4,20},{5,69},{6,22},{7,71},{8,24},{9,... | collective-permute-start | bytes 786440 | tf_op jit(solution)/shard_map/ppermute | solution.py:264
  43.2 3.6 %collective-permute-start.8 = (bf16[256,256]{1,0:T(8,128)(2,1)S(1)}, bf16[256,256]{1,0:T(8,128)(2,1)S(1)}, u32[]{:S(2)}, u32[]{:S(2)}) collective-permute-start(bf16[256,256]{1,0:T(8,128)(2,1)S(1)} %get-tuple-element.43), channel_id=1, source_target_pairs={{0,64},{1,17},{2,66},{3,19},{4,68},{5,21},{6,70},{7,23},{8,72},{9,... | collective-permute-start | bytes 393224 | tf_op jit(solution)/shard_map/ppermute | solution.py:264
  48.2 2.7 %collective-permute-done.8.refs_2_ = bf16[256,256]{1,0:T(8,128)(2,1)S(1)} collective-permute-done((bf16[256,256]{1,0:T(8,128)(2,1)S(1)}, bf16[256,256]{1,0:T(8,128)(2,1)S(1)}, u32[]{:S(2)}, u32[]{:S(2)}) %collective-permute-start.8) | collective-permute-done | bytes 131104 | tf_op jit(solution)/shard_map/ppermute | solution.py:264
  60.8 2.6 %collective-permute-start.24 = (bf16[784,256]{1,0:T(8,128)(2,1)S(1)}, bf16[784,256]{1,0:T(8,128)(2,1)S(1)}, u32[]{:S(2)}, u32[]{:S(2)}) collective-permute-start(bf16[784,256]{1,0:T(8,128)(2,1)S(1)} %shard_map.138), channel_id=1, source_target_pairs={{0,96},{1,25},{2,98},{3,27},{4,100},{5,29},{6,102},{7,31},{8,104},... | collective-permute-start | bytes 1204232 | tf_op jit(solution)/shard_map/ppermute | solution.py:264
  65.3 2.7 %collective-permute-start.21 = (bf16[272,256]{1,0:T(8,128)(2,1)S(1)}, bf16[272,256]{1,0:T(8,128)(2,1)S(1)}, u32[]{:S(2)}, u32[]{:S(2)}) collective-permute-start(bf16[272,256]{1,0:T(8,128)(2,1)S(1)} %get-tuple-element.50.refs_0_), channel_id=1, source_target_pairs={{0,96},{1,25},{2,98},{3,27},{4,100},{5,29},{6,102},{7,31},{8,104},... | collective-permute-start | bytes 417800 | tf_op jit(solution)/shard_map/ppermute | solution.py:264
  67.9 6.9 %collective-permute-done.21.refs_6_ = bf16[272,256]{1,0:T(8,128)(2,1)S(1)} collective-permute-done((bf16[272,256]{1,0:T(8,128)(2,1)S(1)}, bf16[272,256]{1,0:T(8,128)(2,1)S(1)}, u32[]{:S(2)}, u32[]{:S(2)}) %collective-permute-start.21) | collective-permute-done | bytes 139296 | tf_op jit(solution)/shard_map/ppermute | solution.py:264
  74.9 2.9 %collective-permute-start.19 = (bf16[272,256]{1,0:T(8,128)(2,1)S(1)}, bf16[272,256]{1,0:T(8,128)(2,1)S(1)}, u32[]{:S(2)}, u32[]{:S(2)}) collective-permute-start(bf16[272,256]{1,0:T(8,128)(2,1)S(1)} %get-tuple-element.50.refs_0_), channel_id=1, source_target_pairs={{0,32},{1,9},{2,34},{3,11},{4,36},{5,13},{6,38},{7,15},{8,40},{9,1... | collective-permute-start | bytes 417800 | tf_op jit(solution)/shard_map/ppermute | solution.py:264
  77.8 3.8 %collective-permute-done.19.refs_4_ = bf16[272,256]{1,0:T(8,128)(2,1)S(1)} collective-permute-done((bf16[272,256]{1,0:T(8,128)(2,1)S(1)}, bf16[272,256]{1,0:T(8,128)(2,1)S(1)}, u32[]{:S(2)}, u32[]{:S(2)}) %collective-permute-start.19) | collective-permute-done | bytes 139296 | tf_op jit(solution)/shard_map/ppermute | solution.py:264
  81.5 2.3 %shard_map.140 = f32[4,264,256]{2,1,0:T(8,128)S(1)} custom-call(bf16[128,256,256]{2,1,0:T(8,128)(2,1)S(1)} %dense.1, bf16[272,256]{1,0:T(8,128)(2,1)S(1)} %get-tuple-element.50.refs_0_, bf16[272,256]{1,0:T(8,128)(2,1)S(1)} %collective-permute-done.16.refs_1_, bf16[272,256]{1,0:T(8,128)(2,1)S(1)} %collective-permute-done.17.refs_2_, ...), custom_call_target="tpu_custom_call" | custom-call | flops 2147483648 | bytes 8388608 | tf_op jit(solution)/shard_map/pallas_call | solution.py:105
  83.9 4.7 %collective-permute-start.25 = (f32[4,264,256]{2,1,0:T(8,128)S(1)}, f32[4,264,256]{2,1,0:T(8,128)S(1)}, u32[]{:S(2)}, u32[]{:S(2)}) collective-permute-start(f32[4,264,256]{2,1,0:T(8,128)S(1)} %shard_map.140), channel_id=1, source_target_pairs={{0,1},{1,0},{2,3},{3,2},{4,5},{5,4},{6,7},{7,6},{8,9},{9,8},{10,11... | collective-permute-start | bytes 3244040 | tf_op jit(solution)/shard_map/ppermute | solution.py:264
  88.5 2.3 %shard_map.139.refs_0_ = f32[4,264,256]{2,1,0:T(8,128)S(1)} custom-call(bf16[128,256,256]{2,1,0:T(8,128)(2,1)S(1)} %dense.1, bf16[272,256]{1,0:T(8,128)(2,1)S(1)} %get-tuple-element.50.refs_0_, bf16[272,256]{1,0:T(8,128)(2,1)S(1)} %collective-permute-done.16.refs_1_, bf16[272,256]{1,0:T(8,128)(2,1)S(1)} %collective-permute-done.17.refs_2_, ...), custom_call_target="tpu_custom_call" | custom-call | flops 2147483648 | bytes 8388608 | tf_op jit(solution)/shard_map/pallas_call | solution.py:105
  91.1 2.2 %collective-permute-start.26 = (bf16[272,256]{1,0:T(8,128)(2,1)S(1)}, bf16[272,256]{1,0:T(8,128)(2,1)S(1)}, u32[]{:S(2)}, u32[]{:S(2)}) collective-permute-start(bf16[272,256]{1,0:T(8,128)(2,1)S(1)} %get-tuple-element.52), channel_id=1, source_target_pairs={{0,2},{1,3},{2,4},{3,5},{4,6},{5,7},{6,0},{7,1},{8,10},{9,11},{10,... | collective-permute-start | bytes 417800 | tf_op jit(solution)/shard_map/ppermute | solution.py:264
  97.3 3.8 %collective-permute-done.27.refs_2_ = bf16[272,256]{1,0:T(8,128)(2,1)S(1)} collective-permute-done((bf16[272,256]{1,0:T(8,128)(2,1)S(1)}, bf16[272,256]{1,0:T(8,128)(2,1)S(1)}, u32[]{:S(2)}, u32[]{:S(2)}) %collective-permute-start.27) | collective-permute-done | bytes 139296 | tf_op jit(solution)/shard_map/ppermute | solution.py:264
  101.3 2.6 %collective-permute-start.31 = (bf16[272,256]{1,0:T(8,128)(2,1)S(1)}, bf16[272,256]{1,0:T(8,128)(2,1)S(1)}, u32[]{:S(2)}, u32[]{:S(2)}) collective-permute-start(bf16[272,256]{1,0:T(8,128)(2,1)S(1)} %get-tuple-element.55.refs_0_), channel_id=1, source_target_pairs={{0,6},{1,7},{2,0},{3,1},{4,2},{5,3},{6,4},{7,5},{8,14},{9,15},{10,... | collective-permute-start | bytes 417800 | tf_op jit(solution)/shard_map/ppermute | solution.py:264
  107.7 3.1 %collective-permute-start.35 = (bf16[272,256]{1,0:T(8,128)(2,1)S(1)}, bf16[272,256]{1,0:T(8,128)(2,1)S(1)}, u32[]{:S(2)}, u32[]{:S(2)}) collective-permute-start(bf16[272,256]{1,0:T(8,128)(2,1)S(1)} %collective-permute-done.31.refs_3_), channel_id=1, source_target_pairs={{0,1},{1,0},{2,3},{3,2},{4,5},{5,4},{6,7},{7,6},{8,9},{9,8},{10,11... | collective-permute-start | bytes 417800 | tf_op jit(solution)/shard_map/ppermute | solution.py:264
  124.0 5.0 %collective-permute-done.39.refs_2_ = bf16[784,256]{1,0:T(8,128)(2,1)S(1)} collective-permute-done((bf16[784,256]{1,0:T(8,128)(2,1)S(1)}, bf16[784,256]{1,0:T(8,128)(2,1)S(1)}, u32[]{:S(2)}, u32[]{:S(2)}) %collective-permute-start.39) | collective-permute-done | bytes 401440 | tf_op jit(solution)/shard_map/ppermute | solution.py:264
  131.0 2.9 %collective-permute-start.43 = (f32[264,256]{1,0:T(8,128)S(1)}, f32[264,256]{1,0:T(8,128)S(1)}, u32[]{:S(2)}, u32[]{:S(2)}) collective-permute-start(f32[264,256]{1,0:T(8,128)S(1)} %get-tuple-element.63), channel_id=1, source_target_pairs={{0,16},{1,65},{2,18},{3,67},{4,20},{5,69},{6,22},{7,71},{8,24},{9,... | collective-permute-start | bytes 811016 | tf_op jit(solution)/shard_map/ppermute | solution.py:264
  134.6 2.6 %collective-permute-start.37 = (bf16[256,256]{1,0:T(8,128)(2,1)S(1)}, bf16[256,256]{1,0:T(8,128)(2,1)S(1)}, u32[]{:S(2)}, u32[]{:S(2)}) collective-permute-start(bf16[256,256]{1,0:T(8,128)(2,1)S(1)} %get-tuple-element.58), channel_id=1, source_target_pairs={{0,64},{1,17},{2,66},{3,19},{4,68},{5,21},{6,70},{7,23},{8,72},{9,... | collective-permute-start | bytes 393224 | tf_op jit(solution)/shard_map/ppermute | solution.py:264
  137.2 7.8 %collective-permute-done.36.refs_1_ = bf16[256,256]{1,0:T(8,128)(2,1)S(1)} collective-permute-done((bf16[256,256]{1,0:T(8,128)(2,1)S(1)}, bf16[256,256]{1,0:T(8,128)(2,1)S(1)}, u32[]{:S(2)}, u32[]{:S(2)}) %collective-permute-start.36) | collective-permute-done | bytes 131104 | tf_op jit(solution)/shard_map/ppermute | solution.py:264
  145.0 3.8 %collective-permute-done.38.refs_3_ = bf16[256,256]{1,0:T(8,128)(2,1)S(1)} collective-permute-done((bf16[256,256]{1,0:T(8,128)(2,1)S(1)}, bf16[256,256]{1,0:T(8,128)(2,1)S(1)}, u32[]{:S(2)}, u32[]{:S(2)}) %collective-permute-start.38) | collective-permute-done | bytes 131104 | tf_op jit(solution)/shard_map/ppermute | solution.py:264
  158.8 2.3 %collective-permute-start.50 = (bf16[256,256]{1,0:T(8,128)(2,1)S(1)}, bf16[256,256]{1,0:T(8,128)(2,1)S(1)}, u32[]{:S(2)}, u32[]{:S(2)}) collective-permute-start(bf16[256,256]{1,0:T(8,128)(2,1)S(1)} %get-tuple-element.69.refs_0_), channel_id=1, source_target_pairs={{0,96},{1,25},{2,98},{3,27},{4,100},{5,29},{6,102},{7,31},{8,104},... | collective-permute-start | bytes 393224 | tf_op jit(solution)/shard_map/ppermute | solution.py:264
  162.5 7.2 %collective-permute-done.50.refs_6_ = bf16[256,256]{1,0:T(8,128)(2,1)S(1)} collective-permute-done((bf16[256,256]{1,0:T(8,128)(2,1)S(1)}, bf16[256,256]{1,0:T(8,128)(2,1)S(1)}, u32[]{:S(2)}, u32[]{:S(2)}) %collective-permute-start.50) | collective-permute-done | bytes 131104 | tf_op jit(solution)/shard_map/ppermute | solution.py:264
  171.9 3.2 %collective-permute-done.48.refs_4_ = bf16[256,256]{1,0:T(8,128)(2,1)S(1)} collective-permute-done((bf16[256,256]{1,0:T(8,128)(2,1)S(1)}, bf16[256,256]{1,0:T(8,128)(2,1)S(1)}, u32[]{:S(2)}, u32[]{:S(2)}) %collective-permute-start.48) | collective-permute-done | bytes 131104 | tf_op jit(solution)/shard_map/ppermute | solution.py:264
  175.1 2.3 %shard_map.151 = f32[4,256,256]{2,1,0:T(8,128)S(1)} custom-call(bf16[128,256,256]{2,1,0:T(8,128)(2,1)S(1)} %dense.1, bf16[256,256]{1,0:T(8,128)(2,1)S(1)} %get-tuple-element.69.refs_0_, bf16[256,256]{1,0:T(8,128)(2,1)S(1)} %collective-permute-done.45.refs_1_, bf16[256,256]{1,0:T(8,128)(2,1)S(1)} %collective-permute-done.46.refs_2_, ...), custom_call_target="tpu_custom_call" | custom-call | flops 2147483648 | bytes 8388608 | tf_op jit(solution)/shard_map/pallas_call | solution.py:105
  177.4 4.7 %collective-permute-start.54 = (f32[4,256,256]{2,1,0:T(8,128)S(1)}, f32[4,256,256]{2,1,0:T(8,128)S(1)}, u32[]{:S(2)}, u32[]{:S(2)}) collective-permute-start(f32[4,256,256]{2,1,0:T(8,128)S(1)} %shard_map.151), channel_id=1, source_target_pairs={{0,1},{1,0},{2,3},{3,2},{4,5},{5,4},{6,7},{7,6},{8,9},{9,8},{10,11... | collective-permute-start | bytes 3145736 | tf_op jit(solution)/shard_map/ppermute | solution.py:264
  182.1 2.3 %shard_map.150.refs_0_ = f32[4,256,256]{2,1,0:T(8,128)S(1)} custom-call(bf16[128,256,256]{2,1,0:T(8,128)(2,1)S(1)} %dense.1, bf16[256,256]{1,0:T(8,128)(2,1)S(1)} %get-tuple-element.69.refs_0_, bf16[256,256]{1,0:T(8,128)(2,1)S(1)} %collective-permute-done.45.refs_1_, bf16[256,256]{1,0:T(8,128)(2,1)S(1)} %collective-permute-done.46.refs_2_, ...), custom_call_target="tpu_custom_call" | custom-call | flops 2147483648 | bytes 8388608 | tf_op jit(solution)/shard_map/pallas_call | solution.py:105
  187.6 5.8 %collective-permute-done.55.refs_1_ = bf16[256,256]{1,0:T(8,128)(2,1)S(1)} collective-permute-done((bf16[256,256]{1,0:T(8,128)(2,1)S(1)}, bf16[256,256]{1,0:T(8,128)(2,1)S(1)}, u32[]{:S(2)}, u32[]{:S(2)}) %collective-permute-start.55) | collective-permute-done | bytes 131104 | tf_op jit(solution)/shard_map/ppermute | solution.py:264
  (132 shorter events, 74.3 us)
Async XLA Ops:
  1.7 17.5 %collective-permute-start.2 = (bf16[256,256]{1,0:T(8,128)(2,1)S(1)}, bf16[256,256]{1,0:T(8,128)(2,1)S(1)}, u32[]{:S(2)}, u32[]{:S(2)}) collective-permute-start(bf16[256,256]{1,0:T(8,128)(2,1)S(1)} %shard_map.131.refs_0_), channel_id=1, source_target_pairs={{0,6},{1,7},{2,0},{3,1},{4,2},{5,3},{6,4},{7,5},{8,14},{9,15},{10,... | collective-permute-start | bytes 393224 | tf_op jit(solution)/shard_map/ppermute | solution.py:264
  5.1 14.2 %collective-permute-start.1 = (bf16[256,256]{1,0:T(8,128)(2,1)S(1)}, bf16[256,256]{1,0:T(8,128)(2,1)S(1)}, u32[]{:S(2)}, u32[]{:S(2)}) collective-permute-start(bf16[256,256]{1,0:T(8,128)(2,1)S(1)} %shard_map.131.refs_0_), channel_id=1, source_target_pairs={{0,4},{1,5},{2,6},{3,7},{4,0},{5,1},{6,2},{7,3},{8,12},{9,13},{10,... | collective-permute-start | bytes 393224 | tf_op jit(solution)/shard_map/ppermute | solution.py:264
  5.6 14.1 %collective-permute-start = (bf16[256,256]{1,0:T(8,128)(2,1)S(1)}, bf16[256,256]{1,0:T(8,128)(2,1)S(1)}, u32[]{:S(2)}, u32[]{:S(2)}) collective-permute-start(bf16[256,256]{1,0:T(8,128)(2,1)S(1)} %shard_map.131.refs_0_), channel_id=1, source_target_pairs={{0,2},{1,3},{2,4},{3,5},{4,6},{5,7},{6,0},{7,1},{8,10},{9,11},{10,... | collective-permute-start | bytes 393224 | tf_op jit(solution)/shard_map/ppermute | solution.py:264
  22.0 10.7 %collective-permute-start.10 = (bf16[768,256]{1,0:T(8,128)(2,1)S(1)}, bf16[768,256]{1,0:T(8,128)(2,1)S(1)}, u32[]{:S(2)}, u32[]{:S(2)}) collective-permute-start(bf16[768,256]{1,0:T(8,128)(2,1)S(1)} %shard_map.133), channel_id=1, source_target_pairs={{0,32},{1,9},{2,34},{3,11},{4,36},{5,13},{6,38},{7,15},{8,40},{9,1... | collective-permute-start | bytes 1179656 | tf_op jit(solution)/shard_map/ppermute | solution.py:264
  24.9 11.6 %collective-permute-start.11 = (bf16[768,256]{1,0:T(8,128)(2,1)S(1)}, bf16[768,256]{1,0:T(8,128)(2,1)S(1)}, u32[]{:S(2)}, u32[]{:S(2)}) collective-permute-start(bf16[768,256]{1,0:T(8,128)(2,1)S(1)} %shard_map.134), channel_id=1, source_target_pairs={{0,64},{1,17},{2,66},{3,19},{4,68},{5,21},{6,70},{7,23},{8,72},{9,... | collective-permute-start | bytes 1179656 | tf_op jit(solution)/shard_map/ppermute | solution.py:264
  29.0 8.1 %collective-permute-start.12 = (bf16[768,256]{1,0:T(8,128)(2,1)S(1)}, bf16[768,256]{1,0:T(8,128)(2,1)S(1)}, u32[]{:S(2)}, u32[]{:S(2)}) collective-permute-start(bf16[768,256]{1,0:T(8,128)(2,1)S(1)} %shard_map.135), channel_id=1, source_target_pairs={{0,96},{1,25},{2,98},{3,27},{4,100},{5,29},{6,102},{7,31},{8,104},... | collective-permute-start | bytes 1179656 | tf_op jit(solution)/shard_map/ppermute | solution.py:264
  32.0 14.9 %collective-permute-start.7 = (bf16[256,256]{1,0:T(8,128)(2,1)S(1)}, bf16[256,256]{1,0:T(8,128)(2,1)S(1)}, u32[]{:S(2)}, u32[]{:S(2)}) collective-permute-start(bf16[256,256]{1,0:T(8,128)(2,1)S(1)} %get-tuple-element.42), channel_id=1, source_target_pairs={{0,32},{1,9},{2,34},{3,11},{4,36},{5,13},{6,38},{7,15},{8,40},{9,1... | collective-permute-start | bytes 393224 | tf_op jit(solution)/shard_map/ppermute | solution.py:264
  37.7 14.7 %collective-permute-start.13 = (f32[256,256]{1,0:T(8,128)S(1)}, f32[256,256]{1,0:T(8,128)S(1)}, u32[]{:S(2)}, u32[]{:S(2)}) collective-permute-start(f32[256,256]{1,0:T(8,128)S(1)} %get-tuple-element.47), channel_id=1, source_target_pairs={{0,8},{1,33},{2,10},{3,35},{4,12},{5,37},{6,14},{7,39},{8,16},{9,4... | collective-permute-start | bytes 786440 | tf_op jit(solution)/shard_map/ppermute | solution.py:264
  39.3 13.2 %collective-permute-start.14 = (f32[256,256]{1,0:T(8,128)S(1)}, f32[256,256]{1,0:T(8,128)S(1)}, u32[]{:S(2)}, u32[]{:S(2)}) collective-permute-start(f32[256,256]{1,0:T(8,128)S(1)} %get-tuple-element.48), channel_id=1, source_target_pairs={{0,16},{1,65},{2,18},{3,67},{4,20},{5,69},{6,22},{7,71},{8,24},{9,... | collective-permute-start | bytes 786440 | tf_op jit(solution)/shard_map/ppermute | solution.py:264
  41.9 10.6 %collective-permute-start.15 = (f32[256,256]{1,0:T(8,128)S(1)}, f32[256,256]{1,0:T(8,128)S(1)}, u32[]{:S(2)}, u32[]{:S(2)}) collective-permute-start(f32[256,256]{1,0:T(8,128)S(1)} %get-tuple-element.49), channel_id=1, source_target_pairs={{0,24},{1,97},{2,26},{3,99},{4,28},{5,101},{6,30},{7,103},{8,0},{9... | collective-permute-start | bytes 786440 | tf_op jit(solution)/shard_map/ppermute | solution.py:264
  60.8 20.7 %collective-permute-start.24 = (bf16[784,256]{1,0:T(8,128)(2,1)S(1)}, bf16[784,256]{1,0:T(8,128)(2,1)S(1)}, u32[]{:S(2)}, u32[]{:S(2)}) collective-permute-start(bf16[784,256]{1,0:T(8,128)(2,1)S(1)} %shard_map.138), channel_id=1, source_target_pairs={{0,96},{1,25},{2,98},{3,27},{4,100},{5,29},{6,102},{7,31},{8,104},... | collective-permute-start | bytes 1204232 | tf_op jit(solution)/shard_map/ppermute | solution.py:264
  63.4 18.1 %collective-permute-start.23 = (bf16[784,256]{1,0:T(8,128)(2,1)S(1)}, bf16[784,256]{1,0:T(8,128)(2,1)S(1)}, u32[]{:S(2)}, u32[]{:S(2)}) collective-permute-start(bf16[784,256]{1,0:T(8,128)(2,1)S(1)} %shard_map.138), channel_id=1, source_target_pairs={{0,64},{1,17},{2,66},{3,19},{4,68},{5,21},{6,70},{7,23},{8,72},{9,... | collective-permute-start | bytes 1204232 | tf_op jit(solution)/shard_map/ppermute | solution.py:264
  65.3 16.3 %collective-permute-start.22 = (bf16[784,256]{1,0:T(8,128)(2,1)S(1)}, bf16[784,256]{1,0:T(8,128)(2,1)S(1)}, u32[]{:S(2)}, u32[]{:S(2)}) collective-permute-start(bf16[784,256]{1,0:T(8,128)(2,1)S(1)} %shard_map.138), channel_id=1, source_target_pairs={{0,32},{1,9},{2,34},{3,11},{4,36},{5,13},{6,38},{7,15},{8,40},{9,1... | collective-permute-start | bytes 1204232 | tf_op jit(solution)/shard_map/ppermute | solution.py:264
  65.3 9.6 %collective-permute-start.21 = (bf16[272,256]{1,0:T(8,128)(2,1)S(1)}, bf16[272,256]{1,0:T(8,128)(2,1)S(1)}, u32[]{:S(2)}, u32[]{:S(2)}) collective-permute-start(bf16[272,256]{1,0:T(8,128)(2,1)S(1)} %get-tuple-element.50.refs_0_), channel_id=1, source_target_pairs={{0,96},{1,25},{2,98},{3,27},{4,100},{5,29},{6,102},{7,31},{8,104},... | collective-permute-start | bytes 417800 | tf_op jit(solution)/shard_map/ppermute | solution.py:264
  67.9 9.8 %collective-permute-start.20 = (bf16[272,256]{1,0:T(8,128)(2,1)S(1)}, bf16[272,256]{1,0:T(8,128)(2,1)S(1)}, u32[]{:S(2)}, u32[]{:S(2)}) collective-permute-start(bf16[272,256]{1,0:T(8,128)(2,1)S(1)} %get-tuple-element.50.refs_0_), channel_id=1, source_target_pairs={{0,64},{1,17},{2,66},{3,19},{4,68},{5,21},{6,70},{7,23},{8,72},{9,... | collective-permute-start | bytes 417800 | tf_op jit(solution)/shard_map/ppermute | solution.py:264
  104.8 8.8 %collective-permute-start.29 = (bf16[272,256]{1,0:T(8,128)(2,1)S(1)}, bf16[272,256]{1,0:T(8,128)(2,1)S(1)}, u32[]{:S(2)}, u32[]{:S(2)}) collective-permute-start(bf16[272,256]{1,0:T(8,128)(2,1)S(1)} %get-tuple-element.55.refs_0_), channel_id=1, source_target_pairs={{0,2},{1,3},{2,4},{3,5},{4,6},{5,7},{6,0},{7,1},{8,10},{9,11},{10,... | collective-permute-start | bytes 417800 | tf_op jit(solution)/shard_map/ppermute | solution.py:264
  104.8 9.7 %collective-permute-start.32 = (bf16[272,256]{1,0:T(8,128)(2,1)S(1)}, bf16[272,256]{1,0:T(8,128)(2,1)S(1)}, u32[]{:S(2)}, u32[]{:S(2)}) collective-permute-start(bf16[272,256]{1,0:T(8,128)(2,1)S(1)} %get-tuple-element.55.refs_0_), channel_id=1, source_target_pairs={{0,1},{1,0},{2,3},{3,2},{4,5},{5,4},{6,7},{7,6},{8,9},{9,8},{10,11... | collective-permute-start | bytes 417800 | tf_op jit(solution)/shard_map/ppermute | solution.py:264
  116.5 12.6 %collective-permute-start.39 = (bf16[784,256]{1,0:T(8,128)(2,1)S(1)}, bf16[784,256]{1,0:T(8,128)(2,1)S(1)}, u32[]{:S(2)}, u32[]{:S(2)}) collective-permute-start(bf16[784,256]{1,0:T(8,128)(2,1)S(1)} %shard_map.144), channel_id=1, source_target_pairs={{0,32},{1,9},{2,34},{3,11},{4,36},{5,13},{6,38},{7,15},{8,40},{9,1... | collective-permute-start | bytes 1204232 | tf_op jit(solution)/shard_map/ppermute | solution.py:264
  117.5 11.5 %collective-permute-start.40 = (bf16[784,256]{1,0:T(8,128)(2,1)S(1)}, bf16[784,256]{1,0:T(8,128)(2,1)S(1)}, u32[]{:S(2)}, u32[]{:S(2)}) collective-permute-start(bf16[784,256]{1,0:T(8,128)(2,1)S(1)} %shard_map.145), channel_id=1, source_target_pairs={{0,64},{1,17},{2,66},{3,19},{4,68},{5,21},{6,70},{7,23},{8,72},{9,... | collective-permute-start | bytes 1204232 | tf_op jit(solution)/shard_map/ppermute | solution.py:264
  120.1 10.7 %collective-permute-start.41 = (bf16[784,256]{1,0:T(8,128)(2,1)S(1)}, bf16[784,256]{1,0:T(8,128)(2,1)S(1)}, u32[]{:S(2)}, u32[]{:S(2)}) collective-permute-start(bf16[784,256]{1,0:T(8,128)(2,1)S(1)} %shard_map.146), channel_id=1, source_target_pairs={{0,96},{1,25},{2,98},{3,27},{4,100},{5,29},{6,102},{7,31},{8,104},... | collective-permute-start | bytes 1204232 | tf_op jit(solution)/shard_map/ppermute | solution.py:264
  130.9 17.8 %collective-permute-start.42 = (f32[264,256]{1,0:T(8,128)S(1)}, f32[264,256]{1,0:T(8,128)S(1)}, u32[]{:S(2)}, u32[]{:S(2)}) collective-permute-start(f32[264,256]{1,0:T(8,128)S(1)} %get-tuple-element.62), channel_id=1, source_target_pairs={{0,8},{1,33},{2,10},{3,35},{4,12},{5,37},{6,14},{7,39},{8,16},{9,4... | collective-permute-start | bytes 811016 | tf_op jit(solution)/shard_map/ppermute | solution.py:264
  131.0 17.8 %collective-permute-start.43 = (f32[264,256]{1,0:T(8,128)S(1)}, f32[264,256]{1,0:T(8,128)S(1)}, u32[]{:S(2)}, u32[]{:S(2)}) collective-permute-start(f32[264,256]{1,0:T(8,128)S(1)} %get-tuple-element.63), channel_id=1, source_target_pairs={{0,16},{1,65},{2,18},{3,67},{4,20},{5,69},{6,22},{7,71},{8,24},{9,... | collective-permute-start | bytes 811016 | tf_op jit(solution)/shard_map/ppermute | solution.py:264
  133.9 14.9 %collective-permute-start.44 = (f32[264,256]{1,0:T(8,128)S(1)}, f32[264,256]{1,0:T(8,128)S(1)}, u32[]{:S(2)}, u32[]{:S(2)}) collective-permute-start(f32[264,256]{1,0:T(8,128)S(1)} %get-tuple-element.64), channel_id=1, source_target_pairs={{0,24},{1,97},{2,26},{3,99},{4,28},{5,101},{6,30},{7,103},{8,0},{9... | collective-permute-start | bytes 811016 | tf_op jit(solution)/shard_map/ppermute | solution.py:264
  133.9 11.0 %collective-permute-start.36 = (bf16[256,256]{1,0:T(8,128)(2,1)S(1)}, bf16[256,256]{1,0:T(8,128)(2,1)S(1)}, u32[]{:S(2)}, u32[]{:S(2)}) collective-permute-start(bf16[256,256]{1,0:T(8,128)(2,1)S(1)} %get-tuple-element.57), channel_id=1, source_target_pairs={{0,32},{1,9},{2,34},{3,11},{4,36},{5,13},{6,38},{7,15},{8,40},{9,1... | collective-permute-start | bytes 393224 | tf_op jit(solution)/shard_map/ppermute | solution.py:264
  134.6 10.4 %collective-permute-start.37 = (bf16[256,256]{1,0:T(8,128)(2,1)S(1)}, bf16[256,256]{1,0:T(8,128)(2,1)S(1)}, u32[]{:S(2)}, u32[]{:S(2)}) collective-permute-start(bf16[256,256]{1,0:T(8,128)(2,1)S(1)} %get-tuple-element.58), channel_id=1, source_target_pairs={{0,64},{1,17},{2,66},{3,19},{4,68},{5,21},{6,70},{7,23},{8,72},{9,... | collective-permute-start | bytes 393224 | tf_op jit(solution)/shard_map/ppermute | solution.py:264
  157.1 18.0 %collective-permute-start.53 = (bf16[768,256]{1,0:T(8,128)(2,1)S(1)}, bf16[768,256]{1,0:T(8,128)(2,1)S(1)}, u32[]{:S(2)}, u32[]{:S(2)}) collective-permute-start(bf16[768,256]{1,0:T(8,128)(2,1)S(1)} %shard_map.149), channel_id=1, source_target_pairs={{0,96},{1,25},{2,98},{3,27},{4,100},{5,29},{6,102},{7,31},{8,104},... | collective-permute-start | bytes 1179656 | tf_op jit(solution)/shard_map/ppermute | solution.py:264
  158.1 17.0 %collective-permute-start.52 = (bf16[768,256]{1,0:T(8,128)(2,1)S(1)}, bf16[768,256]{1,0:T(8,128)(2,1)S(1)}, u32[]{:S(2)}, u32[]{:S(2)}) collective-permute-start(bf16[768,256]{1,0:T(8,128)(2,1)S(1)} %shard_map.149), channel_id=1, source_target_pairs={{0,64},{1,17},{2,66},{3,19},{4,68},{5,21},{6,70},{7,23},{8,72},{9,... | collective-permute-start | bytes 1179656 | tf_op jit(solution)/shard_map/ppermute | solution.py:264
  158.4 16.7 %collective-permute-start.51 = (bf16[768,256]{1,0:T(8,128)(2,1)S(1)}, bf16[768,256]{1,0:T(8,128)(2,1)S(1)}, u32[]{:S(2)}, u32[]{:S(2)}) collective-permute-start(bf16[768,256]{1,0:T(8,128)(2,1)S(1)} %shard_map.149), channel_id=1, source_target_pairs={{0,32},{1,9},{2,34},{3,11},{4,36},{5,13},{6,38},{7,15},{8,40},{9,1... | collective-permute-start | bytes 1179656 | tf_op jit(solution)/shard_map/ppermute | solution.py:264
  158.8 11.0 %collective-permute-start.50 = (bf16[256,256]{1,0:T(8,128)(2,1)S(1)}, bf16[256,256]{1,0:T(8,128)(2,1)S(1)}, u32[]{:S(2)}, u32[]{:S(2)}) collective-permute-start(bf16[256,256]{1,0:T(8,128)(2,1)S(1)} %get-tuple-element.69.refs_0_), channel_id=1, source_target_pairs={{0,96},{1,25},{2,98},{3,27},{4,100},{5,29},{6,102},{7,31},{8,104},... | collective-permute-start | bytes 393224 | tf_op jit(solution)/shard_map/ppermute | solution.py:264
  161.1 10.8 %collective-permute-start.49 = (bf16[256,256]{1,0:T(8,128)(2,1)S(1)}, bf16[256,256]{1,0:T(8,128)(2,1)S(1)}, u32[]{:S(2)}, u32[]{:S(2)}) collective-permute-start(bf16[256,256]{1,0:T(8,128)(2,1)S(1)} %get-tuple-element.69.refs_0_), channel_id=1, source_target_pairs={{0,64},{1,17},{2,66},{3,19},{4,68},{5,21},{6,70},{7,23},{8,72},{9,... | collective-permute-start | bytes 393224 | tf_op jit(solution)/shard_map/ppermute | solution.py:264
  184.6 8.8 %collective-permute-start.55 = (bf16[256,256]{1,0:T(8,128)(2,1)S(1)}, bf16[256,256]{1,0:T(8,128)(2,1)S(1)}, u32[]{:S(2)}, u32[]{:S(2)}) collective-permute-start(bf16[256,256]{1,0:T(8,128)(2,1)S(1)} %get-tuple-element.71), channel_id=1, source_target_pairs={{0,2},{1,3},{2,4},{3,5},{4,6},{5,7},{6,0},{7,1},{8,10},{9,11},{10,... | collective-permute-start | bytes 393224 | tf_op jit(solution)/shard_map/ppermute | solution.py:264
  184.7 8.7 %collective-permute-start.56 = (bf16[256,256]{1,0:T(8,128)(2,1)S(1)}, bf16[256,256]{1,0:T(8,128)(2,1)S(1)}, u32[]{:S(2)}, u32[]{:S(2)}) collective-permute-start(bf16[256,256]{1,0:T(8,128)(2,1)S(1)} %get-tuple-element.72), channel_id=1, source_target_pairs={{0,4},{1,5},{2,6},{3,7},{4,0},{5,1},{6,2},{7,3},{8,12},{9,13},{10,... | collective-permute-start | bytes 393224 | tf_op jit(solution)/shard_map/ppermute | solution.py:264
  (38 other events, 273.2 us)
where the time goes:
time: 195 us
  starting transfers between devices  81.9 us (42%)
  waiting for transfers between devices  76.3 us (39%)
  Pallas kernels  27.8 us (14%)
  local copies, waits for them, and re-layouts  6.88 us (4%)
    ppermute x58, starting transfers between devices, permute(): return lax.ppermute(value, ROW_COL, [(flat(p), flat(q)) for p, q in places])  81.9 us
    ppermute x58, waiting for transfers between devices, permute(): return lax.ppermute(value, ROW_COL, [(flat(p), flat(q)) for p, q in places])  76.3 us
    pallas_call x12, Pallas kernels, multiply(): pl.pallas_call(kernel, out_shape=[jax.ShapeDtypeStruct(*out) for out in o...  19.4 us
    unnamed x24, local copies, waits for them, and re-layouts  6.88 us
    pallas_call x1, Pallas kernels, make_dense(): pl.pallas_call(dense_kernel, out_shape=jax.ShapeDtypeStruct((NR * NC, T,...  5.01 us
  transfers between devices with their start and end apart: 58, of which 30 were waited for; matrix products, arithmetic and copies ran while one was open for 0% of the time, Pallas kernels for 9%

commit v1 on v0

--- a/solution.py
+++ b/solution.py
@@ -57,16 +57,18 @@
 def dense_kernel(rows, cols, count, tiles, dense, table):
     at_y, at_z, at_x, core = (lax.axis_index(name) for name in ROW_COL)
 
+    used = count[0, 0]
+
     def clear(k, carry):
         table[k] = -1
         return carry
 
     def note(slot, carry):
         row, col = rows[0, 0, slot], cols[0, 0, slot]
-        r = ((row // 2 - at_x) & 3) + jnp.where((row & 1) == core, 0, N4)
-        y, z = (col // N4 - at_y) & 3, (col - at_z) & 3
-        big, small = jnp.where(core == 0, y, z), jnp.where(core == 0, z, y)
-        table[r * NC + big * N4 + small] = slot
+        r = ((lax.shift_right_logical(row, 1) - at_x) & 3) + jnp.where((row & 1) == core, 0, N4)
+        y, z = (lax.shift_right_logical(col, 2) - at_y) & 3, (col - at_z) & 3
+        place = r * NC + jnp.where(core == 1, y * N4 + z, z * N4 + y)
+        table[jnp.where(slot < used, place, NR * NC)] = slot
         return carry
 
     def move(k, carry):
@@ -74,9 +76,9 @@
         dense[k] = tiles[0, 0, jnp.maximum(slot, 0)] * jnp.where(slot >= 0, 1.0, 0.0).astype(bf16)
         return carry
 
-    lax.fori_loop(0, NR * NC, clear, 0)
-    lax.fori_loop(0, count[0, 0], note, 0)
-    lax.fori_loop(0, NR * NC, move, 0)
+    lax.fori_loop(0, NR * NC, clear, 0, unroll=16)
+    lax.fori_loop(0, tiles.shape[2], note, 0, unroll=8)
+    lax.fori_loop(0, NR * NC, move, 0, unroll=4)
 
 
 def make_dense(rows, cols, count, tiles):
@@ -85,7 +87,7 @@
         out_shape=jax.ShapeDtypeStruct((NR * NC, T, T), bf16),
         in_specs=[SMEM, SMEM, SMEM, VMEM],
         out_specs=VMEM,
-        scratch_shapes=[pltpu.SMEM((NR * NC,), jnp.int32)],
+        scratch_shapes=[pltpu.SMEM((NR * NC + 8,), jnp.int32)],
         compiler_params=pltpu.CompilerParams(vmem_limit_bytes=4 * MIB),
         name="dense",
     )(rows, cols, count, tiles)
@@ -116,26 +118,40 @@
     return -k % N4
 
 
-def forward(dense, near, firsts, rests, far, extra):
+def tile_rows_of(dense, rows, places):
+    return jnp.concatenate(
+        [jnp.concatenate([dense[r * NC + c] for c in places], axis=1) for r in rows], axis=0
+    )
+
+
+def forward_early(dense, near, firsts):
     def kernel(dense, *refs):
-        near, firsts, rests, out = refs[:N4], refs[N4 : 2 * N4 - 1], refs[2 * N4 - 1 : -1], refs[-1]
+        pieces, out = refs[:-1], refs[-1]
+        places = [back(a) for a in range(N4)] + [back(b) * N4 for b in range(1, N4)]
+        right = jnp.concatenate([piece[:T, :] for piece in pieces], axis=0)
+        for half in range(2):
+            rows = range(half * N4, half * N4 + N4)
+            product = jnp.dot(tile_rows_of(dense, rows, places), right, preferred_element_type=f32)
+            out[half * N4 : half * N4 + N4] = product.reshape(N4, T, T)
+
+    return multiply(kernel, dense, [*near, *firsts], [((NR, T, T), f32)], 7 * NR)[0]
+
+
+def forward_late(dense, early, near, rests, far, extra):
+    def kernel(dense, *refs):
+        early, near, rests, out = refs[0], refs[1 : 1 + N4], refs[1 + N4 : -1], refs[-1]
         if extra:
             total = sum_of_parts(near) + sum_of_parts(rests, REST)
             out[:, T:, :] = jnp.broadcast_to(one_row(total)[None], (N4, WIDE - T, T))
         first = N4 if far else 0
-        places = [back(b) * N4 + back(a) for b in range(N4) for a in range(N4)]
-        left = jnp.concatenate(
-            [jnp.concatenate([dense[(first + k) * NC + c] for c in places], axis=1) for k in range(N4)], axis=0
-        )
-        right = [tile[:T, :] for tile in near]
-        for one, rest in zip(firsts, rests):
-            right += [one[:T, :], rest[:REST, :]]
-        product = jnp.dot(left, jnp.concatenate(right, axis=0), preferred_element_type=f32)
-        out[:, :T, :] = product.reshape(N4, T, T)
-
-    tall = WIDE if extra else T
-    outs = [((N4, tall, T), f32)]
-    return multiply(kernel, dense, [*near, *firsts, *rests], outs, N4 * NC)[0]
+        places = [back(b) * N4 + back(a) for b in range(1, N4) for a in range(1, N4)]
+        left = tile_rows_of(dense, range(first, first + N4), places)
+        right = jnp.concatenate([rest[:REST, :] for rest in rests], axis=0)
+        product = jnp.dot(left, right, preferred_element_type=f32)
+        out[:, :T, :] = product.reshape(N4, T, T) + early[first : first + N4]
+
+    outs = [((N4, WIDE if extra else T, T), f32)]
+    return multiply(kernel, dense, [early, *near, *rests], outs, 9 * N4)[0]
 
 
 def transposed_product(dense, pieces, places):
@@ -281,11 +297,11 @@
 
 
 def to_big(value, k):
+    return permute(value, [(p, along_y(p, k) if p[3] else along_z(p, k)) for p in EVERYONE])
+
+
+def to_small(value, k):
     return permute(value, [(p, along_z(p, k) if p[3] else along_y(p, k)) for p in EVERYONE])
-
-
-def to_small(value, k):
-    return permute(value, [(p, along_y(p, k) if p[3] else along_z(p, k)) for p in EVERYONE])
 
 
 def to_x(value, k):
@@ -296,11 +312,16 @@
     return permute(value, [(p, (*p[:3], 1 - p[3])) for p in EVERYONE])
 
 
-FAR_FIRST = (2, 1, 3)
+FAR_FIRST = (1, 3, 2)
+
+
+START_ORDER = (1, 3, 2)
 
 
 def sent(values, send):
-    arrived = {k: send(values[k - 1], k) for k in FAR_FIRST}
+    arrived = {}
+    for k in START_ORDER:
+        arrived[k] = send(values[k - 1], k)
     return [arrived[k] for k in range(1, N4)]
 
 
@@ -348,8 +369,9 @@
         tall = TALL if extra else T
         (rest,) = call(lambda *refs: rest_kernel(extra, *refs), [((REST + tall - T, T), bf16)], *near)
         rests = sent([rest] * 3, to_big)
-        other = to_other_core(forward(dense, near, firsts, rests, True, extra))
-        mine = forward(dense, near, firsts, rests, False, extra)
+        early = forward_early(dense, near, firsts)
+        other = to_other_core(forward_late(dense, early, near, rests, True, extra))
+        mine = forward_late(dense, early, near, rests, False, extra)
         outs = [((WIDE if extra else T, T), f32)] + [((tall, T), bf16)] * (N4 - 1)
         own, *blocks = call(lambda *refs: join_kernel(extra, *refs), outs, mine, other)
         return [own, *sent(blocks, to_x)]

time: 195 us -> 191 us (0.979)
  starting transfers between devices: 81.9 us -> 79.2 us
    ppermute x58, starting transfers between devices: 81.9 us -> 79.2 us  [permute(): return lax.ppermute(value, ROW_COL, [(flat(p), flat(q)) for p, q in places])]
    pallas_call x1, Pallas kernels: 5.01 us -> 2.87 us  [make_dense(): pl.pallas_call(dense_kernel, out_shape=jax.ShapeDtypeStruct((NR * NC, T,...]
    pallas_call x12 -> x14, Pallas kernels: 19.4 us -> 19.9 us  [multiply(): pl.pallas_call(kernel, out_shape=[jax.ShapeDtypeStruct(*out) for out in o...]
  transfers between devices with their start and end apart: 58 -> 58, of which waited for: 30 -> 29; matrix products, arithmetic and copies ran while one was open for 0% -> 0% of each run, Pallas kernels for 9% -> 10%
where the time goes in v1:
time: 191 us; the launch traced here: 190 us
  starting transfers between devices  79.2 us (41%)
  waiting for transfers between devices  76.4 us (40%)
  Pallas kernels  26.2 us (14%)
  local copies, waits for them, and re-layouts  6.88 us (4%)
    ppermute x58, starting transfers between devices, permute(): return lax.ppermute(value, ROW_COL, [(flat(p), flat(q)) for p, q in places])  79.2 us
    ppermute x58, waiting for transfers between devices, permute(): return lax.ppermute(value, ROW_COL, [(flat(p), flat(q)) for p, q in places])  76.4 us
    pallas_call x14, Pallas kernels, multiply(): pl.pallas_call(kernel, out_shape=[jax.ShapeDtypeStruct(*out) for out in o...  19.9 us
    unnamed x24, local copies, waits for them, and re-layouts  6.88 us
  transfers between devices with their start and end apart: 58, of which 29 were waited for; matrix products, arithmetic and copies ran while one was open for 0% of the time, Pallas kernels for 10%

profile of v1, /device:TPU:1, one launch (start us, length us, event | category | flops | bytes accessed | tf_op | source)
XLA Modules:
  0.0 190.3 jit_solution(14199463807762204804)
XLA Ops:
  1.7 3.4 %collective-permute-start.2 = (bf16[256,256]{1,0:T(8,128)(2,1)S(1)}, bf16[256,256]{1,0:T(8,128)(2,1)S(1)}, u32[]{:S(2)}, u32[]{:S(2)}) collective-permute-start(bf16[256,256]{1,0:T(8,128)(2,1)S(1)} %shard_map.131.refs_0_), channel_id=1, source_target_pairs={{0,6},{1,7},{2,0},{3,1},{4,2},{5,3},{6,4},{7,5},{8,14},{9,15},{10,... | collective-permute-start | bytes 393224 | tf_op jit(solution)/shard_map/ppermute | solution.py:280
  6.8 4.6 %copy-done = bf16[1,1,96,256,256]{4,3,2,1,0:T(8,128)(2,1)S(1)} copy-done((bf16[1,1,96,256,256]{4,3,2,1,0:T(8,128)(2,1)S(1)}, bf16[1,1,96,256,256]{4,3,2,1,0:T(8,128)(2,1)}, u32[]{:S(2)}) %copy-start) | copy-done | bytes 12582936
  12.7 2.9 %dense.1 = bf16[128,256,256]{2,1,0:T(8,128)(2,1)S(1)} custom-call(s32[1,1,96]{2,1,0:T(1,128)S(1)} %copy-done.10, s32[1,1,96]{2,1,0:T(1,128)S(1)} %copy-done.11, s32[1,1]{1,0:T(1,128)S(6)} %copy.14.count, bf16[1,1,96,256,256]{4,3,2,1,0:T(8,128)(2,1)S(1)} %copy-done), custom_call_target="tpu_custom_call" | custom-call | tf_op jit(solution)/shard_map/dense/pallas_call | solution.py:85
  22.4 2.7 %collective-permute-start.11 = (bf16[768,256]{1,0:T(8,128)(2,1)S(1)}, bf16[768,256]{1,0:T(8,128)(2,1)S(1)}, u32[]{:S(2)}, u32[]{:S(2)}) collective-permute-start(bf16[768,256]{1,0:T(8,128)(2,1)S(1)} %shard_map.134), channel_id=1, source_target_pairs={{0,16},{1,65},{2,18},{3,67},{4,20},{5,69},{6,22},{7,71},{8,24},{9,... | collective-permute-start | bytes 1179656 | tf_op jit(solution)/shard_map/ppermute | solution.py:280
  27.3 2.1 %shard_map.132 = (f32[256,256]{1,0:T(8,128)S(1)}, f32[768,256]{1,0:T(8,128)S(1)}, f32[1,256]{1,0:T(1,128)S(1)}, bf16[256,256]{1,0:T(8,128)(2,1)S(1)}, bf16[256,2...) custom-call(bf16[128,256,256]{2,1,0:T(8,128)(2,1)S(1)} %dense.1, bf16[256,256]{1,0:T(8,128)(2,1)S(1)} %shard_map.131.refs_0_, ...), custom_call_target="tpu_custom_call" | custom-call | flops 1879048192 | bytes 7340032 | tf_op jit(solution)/shard_map/pallas_call | solution.py:107
  29.9 3.8 %collective-permute-done.11.refs_3_ = bf16[768,256]{1,0:T(8,128)(2,1)S(1)} collective-permute-done((bf16[768,256]{1,0:T(8,128)(2,1)S(1)}, bf16[768,256]{1,0:T(8,128)(2,1)S(1)}, u32[]{:S(2)}, u32[]{:S(2)}) %collective-permute-start.11) | collective-permute-done | bytes 393248 | tf_op jit(solution)/shard_map/ppermute | solution.py:280
  36.5 3.3 %collective-permute-start.14 = (f32[256,256]{1,0:T(8,128)S(1)}, f32[256,256]{1,0:T(8,128)S(1)}, u32[]{:S(2)}, u32[]{:S(2)}) collective-permute-start(f32[256,256]{1,0:T(8,128)S(1)} %get-tuple-element.48), channel_id=1, source_target_pairs={{0,64},{1,17},{2,66},{3,19},{4,68},{5,21},{6,70},{7,23},{8,72},{9,... | collective-permute-start | bytes 786440 | tf_op jit(solution)/shard_map/ppermute | solution.py:280
  40.5 2.9 %collective-permute-start.8 = (bf16[256,256]{1,0:T(8,128)(2,1)S(1)}, bf16[256,256]{1,0:T(8,128)(2,1)S(1)}, u32[]{:S(2)}, u32[]{:S(2)}) collective-permute-start(bf16[256,256]{1,0:T(8,128)(2,1)S(1)} %get-tuple-element.43), channel_id=1, source_target_pairs={{0,16},{1,65},{2,18},{3,67},{4,20},{5,69},{6,22},{7,71},{8,24},{9,... | collective-permute-start | bytes 393224 | tf_op jit(solution)/shard_map/ppermute | solution.py:280
  45.1 2.4 %collective-permute-done.8.refs_2_ = bf16[256,256]{1,0:T(8,128)(2,1)S(1)} collective-permute-done((bf16[256,256]{1,0:T(8,128)(2,1)S(1)}, bf16[256,256]{1,0:T(8,128)(2,1)S(1)}, u32[]{:S(2)}, u32[]{:S(2)}) %collective-permute-start.8) | collective-permute-done | bytes 131104 | tf_op jit(solution)/shard_map/ppermute | solution.py:280
  47.6 2.5 %collective-permute-done.9.refs_3_ = bf16[256,256]{1,0:T(8,128)(2,1)S(1)} collective-permute-done((bf16[256,256]{1,0:T(8,128)(2,1)S(1)}, bf16[256,256]{1,0:T(8,128)(2,1)S(1)}, u32[]{:S(2)}, u32[]{:S(2)}) %collective-permute-start.9) | collective-permute-done | bytes 131104 | tf_op jit(solution)/shard_map/ppermute | solution.py:280
  50.6 2.6 %collective-permute-start.17 = (bf16[272,256]{1,0:T(8,128)(2,1)S(1)}, bf16[272,256]{1,0:T(8,128)(2,1)S(1)}, u32[]{:S(2)}, u32[]{:S(2)}) collective-permute-start(bf16[272,256]{1,0:T(8,128)(2,1)S(1)} %get-tuple-element.50.refs_0_.refs_1_), channel_id=1, source_target_pairs={{0,64},{1,17},{2,66},{3,19},{4,68},{5,21},{6,70},{7,23},{8,72},{9,... | collective-permute-start | bytes 417800 | tf_op jit(solution)/shard_map/ppermute | solution.py:280
  53.3 2.7 %collective-permute-start.21 = (bf16[272,256]{1,0:T(8,128)(2,1)S(1)}, bf16[272,256]{1,0:T(8,128)(2,1)S(1)}, u32[]{:S(2)}, u32[]{:S(2)}) collective-permute-start(bf16[272,256]{1,0:T(8,128)(2,1)S(1)} %get-tuple-element.50.refs_0_.refs_1_), channel_id=1, source_target_pairs={{0,24},{1,97},{2,26},{3,99},{4,28},{5,101},{6,30},{7,103},{8,0},{9... | collective-permute-start | bytes 417800 | tf_op jit(solution)/shard_map/ppermute | solution.py:280
  56.1 2.6 %collective-permute-done.16.refs_1_.refs_2_ = bf16[272,256]{1,0:T(8,128)(2,1)S(1)} collective-permute-done((bf16[272,256]{1,0:T(8,128)(2,1)S(1)}, bf16[272,256]{1,0:T(8,128)(2,1)S(1)}, u32[]{:S(2)}, u32[]{:S(2)}) %collective-permute-start.16) | collective-permute-done | bytes 139296 | tf_op jit(solution)/shard_map/ppermute | solution.py:280
  58.7 2.8 %collective-permute-start.24 = (bf16[784,256]{1,0:T(8,128)(2,1)S(1)}, bf16[784,256]{1,0:T(8,128)(2,1)S(1)}, u32[]{:S(2)}, u32[]{:S(2)}) collective-permute-start(bf16[784,256]{1,0:T(8,128)(2,1)S(1)} %shard_map.139), channel_id=1, source_target_pairs={{0,24},{1,97},{2,26},{3,99},{4,28},{5,101},{6,30},{7,103},{8,0},{9... | collective-permute-start | bytes 1204232 | tf_op jit(solution)/shard_map/ppermute | solution.py:280
  66.3 9.4 %collective-permute-done.20.refs_5_ = bf16[272,256]{1,0:T(8,128)(2,1)S(1)} collective-permute-done((bf16[272,256]{1,0:T(8,128)(2,1)S(1)}, bf16[272,256]{1,0:T(8,128)(2,1)S(1)}, u32[]{:S(2)}, u32[]{:S(2)}) %collective-permute-start.20) | collective-permute-done | bytes 139296 | tf_op jit(solution)/shard_map/ppermute | solution.py:280
  77.3 2.0 %shard_map.138.refs_0_ = f32[8,256,256]{2,1,0:T(8,128)S(1)} custom-call(bf16[128,256,256]{2,1,0:T(8,128)(2,1)S(1)} %dense.1, bf16[272,256]{1,0:T(8,128)(2,1)S(1)} %get-tuple-element.50.refs_0_.refs_1_, bf16[272,256]{1,0:T(8,128)(2,1)S(1)} %collective-permute-done.16.refs_1_.refs_2_, bf16[272,256]{1,0:T(8,128)(2,1)S(1)} %collective-permute-done.17.refs_2_.refs_3_, ...), custom_call_target="tpu_custom_call" | custom-call | flops 1879048192 | bytes 7340032 | tf_op jit(solution)/shard_map/pallas_call | solution.py:107
  80.8 4.1 %collective-permute-start.25 = (f32[4,264,256]{2,1,0:T(8,128)S(1)}, f32[4,264,256]{2,1,0:T(8,128)S(1)}, u32[]{:S(2)}, u32[]{:S(2)}) collective-permute-start(f32[4,264,256]{2,1,0:T(8,128)S(1)} %shard_map.141), channel_id=1, source_target_pairs={{0,1},{1,0},{2,3},{3,2},{4,5},{5,4},{6,7},{7,6},{8,9},{9,8},{10,11... | collective-permute-start | bytes 3244040 | tf_op jit(solution)/shard_map/ppermute | solution.py:280
  91.5 2.1 %collective-permute-done.26.refs_1_ = bf16[272,256]{1,0:T(8,128)(2,1)S(1)} collective-permute-done((bf16[272,256]{1,0:T(8,128)(2,1)S(1)}, bf16[272,256]{1,0:T(8,128)(2,1)S(1)}, u32[]{:S(2)}, u32[]{:S(2)}) %collective-permute-start.26) | collective-permute-done | bytes 139296 | tf_op jit(solution)/shard_map/ppermute | solution.py:280
  93.6 3.6 %collective-permute-done.27.refs_2_ = bf16[272,256]{1,0:T(8,128)(2,1)S(1)} collective-permute-done((bf16[272,256]{1,0:T(8,128)(2,1)S(1)}, bf16[272,256]{1,0:T(8,128)(2,1)S(1)}, u32[]{:S(2)}, u32[]{:S(2)}) %collective-permute-start.27) | collective-permute-done | bytes 139296 | tf_op jit(solution)/shard_map/ppermute | solution.py:280
  97.4 3.1 %collective-permute-start.31 = (bf16[272,256]{1,0:T(8,128)(2,1)S(1)}, bf16[272,256]{1,0:T(8,128)(2,1)S(1)}, u32[]{:S(2)}, u32[]{:S(2)}) collective-permute-start(bf16[272,256]{1,0:T(8,128)(2,1)S(1)} %get-tuple-element.55.refs_0_), channel_id=1, source_target_pairs={{0,6},{1,7},{2,0},{3,1},{4,2},{5,3},{6,4},{7,5},{8,14},{9,15},{10,... | collective-permute-start | bytes 417800 | tf_op jit(solution)/shard_map/ppermute | solution.py:280
  102.3 3.7 %collective-permute-done.31.refs_3_ = bf16[272,256]{1,0:T(8,128)(2,1)S(1)} collective-permute-done((bf16[272,256]{1,0:T(8,128)(2,1)S(1)}, bf16[272,256]{1,0:T(8,128)(2,1)S(1)}, u32[]{:S(2)}, u32[]{:S(2)}) %collective-permute-start.31) | collective-permute-done | bytes 139296 | tf_op jit(solution)/shard_map/ppermute | solution.py:280
  118.3 2.1 %shard_map.144 = (f32[256,256]{1,0:T(8,128)S(1)}, f32[768,256]{1,0:T(8,128)S(1)}, f32[1,256]{1,0:T(1,128)S(1)}, bf16[256,256]{1,0:T(8,128)(2,1)S(1)}, bf16[256,2...) custom-call(bf16[128,256,256]{2,1,0:T(8,128)(2,1)S(1)} %dense.1, bf16[272,256]{1,0:T(8,128)(2,1)S(1)} %get-tuple-element.55.refs_0_, ...), custom_call_target="tpu_custom_call" | custom-call | flops 1879048192 | bytes 7340032 | tf_op jit(solution)/shard_map/pallas_call | solution.py:107
  120.4 5.3 %collective-permute-done.39.refs_2_ = bf16[784,256]{1,0:T(8,128)(2,1)S(1)} collective-permute-done((bf16[784,256]{1,0:T(8,128)(2,1)S(1)}, bf16[784,256]{1,0:T(8,128)(2,1)S(1)}, u32[]{:S(2)}, u32[]{:S(2)}) %collective-permute-start.39) | collective-permute-done | bytes 401440 | tf_op jit(solution)/shard_map/ppermute | solution.py:280
  129.6 2.0 %collective-permute-start.44 = (f32[264,256]{1,0:T(8,128)S(1)}, f32[264,256]{1,0:T(8,128)S(1)}, u32[]{:S(2)}, u32[]{:S(2)}) collective-permute-start(f32[264,256]{1,0:T(8,128)S(1)} %get-tuple-element.64), channel_id=1, source_target_pairs={{0,96},{1,25},{2,98},{3,27},{4,100},{5,29},{6,102},{7,31},{8,104},... | collective-permute-start | bytes 811016 | tf_op jit(solution)/shard_map/ppermute | solution.py:280
  131.9 2.9 %collective-permute-start.37 = (bf16[256,256]{1,0:T(8,128)(2,1)S(1)}, bf16[256,256]{1,0:T(8,128)(2,1)S(1)}, u32[]{:S(2)}, u32[]{:S(2)}) collective-permute-start(bf16[256,256]{1,0:T(8,128)(2,1)S(1)} %get-tuple-element.58), channel_id=1, source_target_pairs={{0,16},{1,65},{2,18},{3,67},{4,20},{5,69},{6,22},{7,71},{8,24},{9,... | collective-permute-start | bytes 393224 | tf_op jit(solution)/shard_map/ppermute | solution.py:280
  134.8 7.2 %collective-permute-done.36.refs_1_ = bf16[256,256]{1,0:T(8,128)(2,1)S(1)} collective-permute-done((bf16[256,256]{1,0:T(8,128)(2,1)S(1)}, bf16[256,256]{1,0:T(8,128)(2,1)S(1)}, u32[]{:S(2)}, u32[]{:S(2)}) %collective-permute-start.36) | collective-permute-done | bytes 131104 | tf_op jit(solution)/shard_map/ppermute | solution.py:280
  142.1 3.8 %collective-permute-done.38.refs_3_ = bf16[256,256]{1,0:T(8,128)(2,1)S(1)} collective-permute-done((bf16[256,256]{1,0:T(8,128)(2,1)S(1)}, bf16[256,256]{1,0:T(8,128)(2,1)S(1)}, u32[]{:S(2)}, u32[]{:S(2)}) %collective-permute-start.38) | collective-permute-done | bytes 131104 | tf_op jit(solution)/shard_map/ppermute | solution.py:280
  156.0 3.2 %collective-permute-start.49 = (bf16[256,256]{1,0:T(8,128)(2,1)S(1)}, bf16[256,256]{1,0:T(8,128)(2,1)S(1)}, u32[]{:S(2)}, u32[]{:S(2)}) collective-permute-start(bf16[256,256]{1,0:T(8,128)(2,1)S(1)} %get-tuple-element.69.refs_0_.refs_1_), channel_id=1, source_target_pairs={{0,16},{1,65},{2,18},{3,67},{4,20},{5,69},{6,22},{7,71},{8,24},{9,... | collective-permute-start | bytes 393224 | tf_op jit(solution)/shard_map/ppermute | solution.py:280
  159.2 10.1 %collective-permute-done.49.refs_5_ = bf16[256,256]{1,0:T(8,128)(2,1)S(1)} collective-permute-done((bf16[256,256]{1,0:T(8,128)(2,1)S(1)}, bf16[256,256]{1,0:T(8,128)(2,1)S(1)}, u32[]{:S(2)}, u32[]{:S(2)}) %collective-permute-start.49) | collective-permute-done | bytes 131104 | tf_op jit(solution)/shard_map/ppermute | solution.py:280
  170.5 2.1 %shard_map.150.refs_0_ = f32[8,256,256]{2,1,0:T(8,128)S(1)} custom-call(bf16[128,256,256]{2,1,0:T(8,128)(2,1)S(1)} %dense.1, bf16[256,256]{1,0:T(8,128)(2,1)S(1)} %get-tuple-element.69.refs_0_.refs_1_, bf16[256,256]{1,0:T(8,128)(2,1)S(1)} %collective-permute-done.45.refs_1_.refs_2_, bf16[256,256]{1,0:T(8,128)(2,1)S(1)} %collective-permute-done.46.refs_2_.refs_3_, ...), custom_call_target="tpu_custom_call" | custom-call | flops 1879048192 | bytes 7340032 | tf_op jit(solution)/shard_map/pallas_call | solution.py:107
  174.0 3.9 %collective-permute-start.54 = (f32[4,256,256]{2,1,0:T(8,128)S(1)}, f32[4,256,256]{2,1,0:T(8,128)S(1)}, u32[]{:S(2)}, u32[]{:S(2)}) collective-permute-start(f32[4,256,256]{2,1,0:T(8,128)S(1)} %shard_map.153), channel_id=1, source_target_pairs={{0,1},{1,0},{2,3},{3,2},{4,5},{5,4},{6,7},{7,6},{8,9},{9,8},{10,11... | collective-permute-start | bytes 3145736 | tf_op jit(solution)/shard_map/ppermute | solution.py:280
  183.3 5.9 %collective-permute-done.55.refs_1_ = bf16[256,256]{1,0:T(8,128)(2,1)S(1)} collective-permute-done((bf16[256,256]{1,0:T(8,128)(2,1)S(1)}, bf16[256,256]{1,0:T(8,128)(2,1)S(1)}, u32[]{:S(2)}, u32[]{:S(2)}) %collective-permute-start.55) | collective-permute-done | bytes 131104 | tf_op jit(solution)/shard_map/ppermute | solution.py:280
  (134 shorter events, 71.0 us)
Async XLA Ops:
  1.7 15.5 %collective-permute-start.2 = (bf16[256,256]{1,0:T(8,128)(2,1)S(1)}, bf16[256,256]{1,0:T(8,128)(2,1)S(1)}, u32[]{:S(2)}, u32[]{:S(2)}) collective-permute-start(bf16[256,256]{1,0:T(8,128)(2,1)S(1)} %shard_map.131.refs_0_), channel_id=1, source_target_pairs={{0,6},{1,7},{2,0},{3,1},{4,2},{5,3},{6,4},{7,5},{8,14},{9,15},{10,... | collective-permute-start | bytes 393224 | tf_op jit(solution)/shard_map/ppermute | solution.py:280
  5.1 12.2 %collective-permute-start.1 = (bf16[256,256]{1,0:T(8,128)(2,1)S(1)}, bf16[256,256]{1,0:T(8,128)(2,1)S(1)}, u32[]{:S(2)}, u32[]{:S(2)}) collective-permute-start(bf16[256,256]{1,0:T(8,128)(2,1)S(1)} %shard_map.131.refs_0_), channel_id=1, source_target_pairs={{0,4},{1,5},{2,6},{3,7},{4,0},{5,1},{6,2},{7,3},{8,12},{9,13},{10,... | collective-permute-start | bytes 393224 | tf_op jit(solution)/shard_map/ppermute | solution.py:280
  5.6 12.1 %collective-permute-start = (bf16[256,256]{1,0:T(8,128)(2,1)S(1)}, bf16[256,256]{1,0:T(8,128)(2,1)S(1)}, u32[]{:S(2)}, u32[]{:S(2)}) collective-permute-start(bf16[256,256]{1,0:T(8,128)(2,1)S(1)} %shard_map.131.refs_0_), channel_id=1, source_target_pairs={{0,2},{1,3},{2,4},{3,5},{4,6},{5,7},{6,0},{7,1},{8,10},{9,11},{10,... | collective-permute-start | bytes 393224 | tf_op jit(solution)/shard_map/ppermute | solution.py:280
  20.1 9.8 %collective-permute-start.10 = (bf16[768,256]{1,0:T(8,128)(2,1)S(1)}, bf16[768,256]{1,0:T(8,128)(2,1)S(1)}, u32[]{:S(2)}, u32[]{:S(2)}) collective-permute-start(bf16[768,256]{1,0:T(8,128)(2,1)S(1)} %shard_map.133), channel_id=1, source_target_pairs={{0,8},{1,33},{2,10},{3,35},{4,12},{5,37},{6,14},{7,39},{8,16},{9,4... | collective-permute-start | bytes 1179656 | tf_op jit(solution)/shard_map/ppermute | solution.py:280
  22.4 11.3 %collective-permute-start.11 = (bf16[768,256]{1,0:T(8,128)(2,1)S(1)}, bf16[768,256]{1,0:T(8,128)(2,1)S(1)}, u32[]{:S(2)}, u32[]{:S(2)}) collective-permute-start(bf16[768,256]{1,0:T(8,128)(2,1)S(1)} %shard_map.134), channel_id=1, source_target_pairs={{0,16},{1,65},{2,18},{3,67},{4,20},{5,69},{6,22},{7,71},{8,24},{9,... | collective-permute-start | bytes 1179656 | tf_op jit(solution)/shard_map/ppermute | solution.py:280
  29.4 14.0 %collective-permute-start.7 = (bf16[256,256]{1,0:T(8,128)(2,1)S(1)}, bf16[256,256]{1,0:T(8,128)(2,1)S(1)}, u32[]{:S(2)}, u32[]{:S(2)}) collective-permute-start(bf16[256,256]{1,0:T(8,128)(2,1)S(1)} %get-tuple-element.42), channel_id=1, source_target_pairs={{0,8},{1,33},{2,10},{3,35},{4,12},{5,37},{6,14},{7,39},{8,16},{9,4... | collective-permute-start | bytes 393224 | tf_op jit(solution)/shard_map/ppermute | solution.py:280
  34.9 15.2 %collective-permute-start.13 = (f32[256,256]{1,0:T(8,128)S(1)}, f32[256,256]{1,0:T(8,128)S(1)}, u32[]{:S(2)}, u32[]{:S(2)}) collective-permute-start(f32[256,256]{1,0:T(8,128)S(1)} %get-tuple-element.47), channel_id=1, source_target_pairs={{0,32},{1,9},{2,34},{3,11},{4,36},{5,13},{6,38},{7,15},{8,40},{9,1... | collective-permute-start | bytes 786440 | tf_op jit(solution)/shard_map/ppermute | solution.py:280
  36.5 13.6 %collective-permute-start.14 = (f32[256,256]{1,0:T(8,128)S(1)}, f32[256,256]{1,0:T(8,128)S(1)}, u32[]{:S(2)}, u32[]{:S(2)}) collective-permute-start(f32[256,256]{1,0:T(8,128)S(1)} %get-tuple-element.48), channel_id=1, source_target_pairs={{0,64},{1,17},{2,66},{3,19},{4,68},{5,21},{6,70},{7,23},{8,72},{9,... | collective-permute-start | bytes 786440 | tf_op jit(solution)/shard_map/ppermute | solution.py:280
  39.8 10.3 %collective-permute-start.15 = (f32[256,256]{1,0:T(8,128)S(1)}, f32[256,256]{1,0:T(8,128)S(1)}, u32[]{:S(2)}, u32[]{:S(2)}) collective-permute-start(f32[256,256]{1,0:T(8,128)S(1)} %get-tuple-element.49), channel_id=1, source_target_pairs={{0,96},{1,25},{2,98},{3,27},{4,100},{5,29},{6,102},{7,31},{8,104},... | collective-permute-start | bytes 786440 | tf_op jit(solution)/shard_map/ppermute | solution.py:280
  53.3 11.7 %collective-permute-start.21 = (bf16[272,256]{1,0:T(8,128)(2,1)S(1)}, bf16[272,256]{1,0:T(8,128)(2,1)S(1)}, u32[]{:S(2)}, u32[]{:S(2)}) collective-permute-start(bf16[272,256]{1,0:T(8,128)(2,1)S(1)} %get-tuple-element.50.refs_0_.refs_1_), channel_id=1, source_target_pairs={{0,24},{1,97},{2,26},{3,99},{4,28},{5,101},{6,30},{7,103},{8,0},{9... | collective-permute-start | bytes 417800 | tf_op jit(solution)/shard_map/ppermute | solution.py:280
  58.7 20.6 %collective-permute-start.24 = (bf16[784,256]{1,0:T(8,128)(2,1)S(1)}, bf16[784,256]{1,0:T(8,128)(2,1)S(1)}, u32[]{:S(2)}, u32[]{:S(2)}) collective-permute-start(bf16[784,256]{1,0:T(8,128)(2,1)S(1)} %shard_map.139), channel_id=1, source_target_pairs={{0,24},{1,97},{2,26},{3,99},{4,28},{5,101},{6,30},{7,103},{8,0},{9... | collective-permute-start | bytes 1204232 | tf_op jit(solution)/shard_map/ppermute | solution.py:280
  61.5 17.9 %collective-permute-start.23 = (bf16[784,256]{1,0:T(8,128)(2,1)S(1)}, bf16[784,256]{1,0:T(8,128)(2,1)S(1)}, u32[]{:S(2)}, u32[]{:S(2)}) collective-permute-start(bf16[784,256]{1,0:T(8,128)(2,1)S(1)} %shard_map.139), channel_id=1, source_target_pairs={{0,16},{1,65},{2,18},{3,67},{4,20},{5,69},{6,22},{7,71},{8,24},{9,... | collective-permute-start | bytes 1204232 | tf_op jit(solution)/shard_map/ppermute | solution.py:280
  63.1 16.3 %collective-permute-start.22 = (bf16[784,256]{1,0:T(8,128)(2,1)S(1)}, bf16[784,256]{1,0:T(8,128)(2,1)S(1)}, u32[]{:S(2)}, u32[]{:S(2)}) collective-permute-start(bf16[784,256]{1,0:T(8,128)(2,1)S(1)} %shard_map.139), channel_id=1, source_target_pairs={{0,8},{1,33},{2,10},{3,35},{4,12},{5,37},{6,14},{7,39},{8,16},{9,4... | collective-permute-start | bytes 1204232 | tf_op jit(solution)/shard_map/ppermute | solution.py:280
  63.1 12.6 %collective-permute-start.20 = (bf16[272,256]{1,0:T(8,128)(2,1)S(1)}, bf16[272,256]{1,0:T(8,128)(2,1)S(1)}, u32[]{:S(2)}, u32[]{:S(2)}) collective-permute-start(bf16[272,256]{1,0:T(8,128)(2,1)S(1)} %get-tuple-element.50.refs_0_.refs_1_), channel_id=1, source_target_pairs={{0,16},{1,65},{2,18},{3,67},{4,20},{5,69},{6,22},{7,71},{8,24},{9,... | collective-permute-start | bytes 417800 | tf_op jit(solution)/shard_map/ppermute | solution.py:280
  64.9 12.4 %collective-permute-start.19 = (bf16[272,256]{1,0:T(8,128)(2,1)S(1)}, bf16[272,256]{1,0:T(8,128)(2,1)S(1)}, u32[]{:S(2)}, u32[]{:S(2)}) collective-permute-start(bf16[272,256]{1,0:T(8,128)(2,1)S(1)} %get-tuple-element.50.refs_0_.refs_1_), channel_id=1, source_target_pairs={{0,8},{1,33},{2,10},{3,35},{4,12},{5,37},{6,14},{7,39},{8,16},{9,4... | collective-permute-start | bytes 417800 | tf_op jit(solution)/shard_map/ppermute | solution.py:280
  101.3 9.3 %collective-permute-start.29 = (bf16[272,256]{1,0:T(8,128)(2,1)S(1)}, bf16[272,256]{1,0:T(8,128)(2,1)S(1)}, u32[]{:S(2)}, u32[]{:S(2)}) collective-permute-start(bf16[272,256]{1,0:T(8,128)(2,1)S(1)} %get-tuple-element.55.refs_0_), channel_id=1, source_target_pairs={{0,2},{1,3},{2,4},{3,5},{4,6},{5,7},{6,0},{7,1},{8,10},{9,11},{10,... | collective-permute-start | bytes 417800 | tf_op jit(solution)/shard_map/ppermute | solution.py:280
  101.3 9.8 %collective-permute-start.32 = (bf16[272,256]{1,0:T(8,128)(2,1)S(1)}, bf16[272,256]{1,0:T(8,128)(2,1)S(1)}, u32[]{:S(2)}, u32[]{:S(2)}) collective-permute-start(bf16[272,256]{1,0:T(8,128)(2,1)S(1)} %get-tuple-element.55.refs_0_), channel_id=1, source_target_pairs={{0,1},{1,0},{2,3},{3,2},{4,5},{5,4},{6,7},{7,6},{8,9},{9,8},{10,11... | collective-permute-start | bytes 417800 | tf_op jit(solution)/shard_map/ppermute | solution.py:280
  113.1 12.6 %collective-permute-start.39 = (bf16[784,256]{1,0:T(8,128)(2,1)S(1)}, bf16[784,256]{1,0:T(8,128)(2,1)S(1)}, u32[]{:S(2)}, u32[]{:S(2)}) collective-permute-start(bf16[784,256]{1,0:T(8,128)(2,1)S(1)} %shard_map.145), channel_id=1, source_target_pairs={{0,8},{1,33},{2,10},{3,35},{4,12},{5,37},{6,14},{7,39},{8,16},{9,4... | collective-permute-start | bytes 1204232 | tf_op jit(solution)/shard_map/ppermute | solution.py:280
  114.2 11.5 %collective-permute-start.40 = (bf16[784,256]{1,0:T(8,128)(2,1)S(1)}, bf16[784,256]{1,0:T(8,128)(2,1)S(1)}, u32[]{:S(2)}, u32[]{:S(2)}) collective-permute-start(bf16[784,256]{1,0:T(8,128)(2,1)S(1)} %shard_map.146), channel_id=1, source_target_pairs={{0,16},{1,65},{2,18},{3,67},{4,20},{5,69},{6,22},{7,71},{8,24},{9,... | collective-permute-start | bytes 1204232 | tf_op jit(solution)/shard_map/ppermute | solution.py:280
  117.0 10.3 %collective-permute-start.41 = (bf16[784,256]{1,0:T(8,128)(2,1)S(1)}, bf16[784,256]{1,0:T(8,128)(2,1)S(1)}, u32[]{:S(2)}, u32[]{:S(2)}) collective-permute-start(bf16[784,256]{1,0:T(8,128)(2,1)S(1)} %shard_map.147), channel_id=1, source_target_pairs={{0,24},{1,97},{2,26},{3,99},{4,28},{5,101},{6,30},{7,103},{8,0},{9... | collective-permute-start | bytes 1204232 | tf_op jit(solution)/shard_map/ppermute | solution.py:280
  127.6 18.3 %collective-permute-start.42 = (f32[264,256]{1,0:T(8,128)S(1)}, f32[264,256]{1,0:T(8,128)S(1)}, u32[]{:S(2)}, u32[]{:S(2)}) collective-permute-start(f32[264,256]{1,0:T(8,128)S(1)} %get-tuple-element.62), channel_id=1, source_target_pairs={{0,32},{1,9},{2,34},{3,11},{4,36},{5,13},{6,38},{7,15},{8,40},{9,1... | collective-permute-start | bytes 811016 | tf_op jit(solution)/shard_map/ppermute | solution.py:280
  128.1 17.8 %collective-permute-start.43 = (f32[264,256]{1,0:T(8,128)S(1)}, f32[264,256]{1,0:T(8,128)S(1)}, u32[]{:S(2)}, u32[]{:S(2)}) collective-permute-start(f32[264,256]{1,0:T(8,128)S(1)} %get-tuple-element.63), channel_id=1, source_target_pairs={{0,64},{1,17},{2,66},{3,19},{4,68},{5,21},{6,70},{7,23},{8,72},{9,... | collective-permute-start | bytes 811016 | tf_op jit(solution)/shard_map/ppermute | solution.py:280
  129.6 16.3 %collective-permute-start.44 = (f32[264,256]{1,0:T(8,128)S(1)}, f32[264,256]{1,0:T(8,128)S(1)}, u32[]{:S(2)}, u32[]{:S(2)}) collective-permute-start(f32[264,256]{1,0:T(8,128)S(1)} %get-tuple-element.64), channel_id=1, source_target_pairs={{0,96},{1,25},{2,98},{3,27},{4,100},{5,29},{6,102},{7,31},{8,104},... | collective-permute-start | bytes 811016 | tf_op jit(solution)/shard_map/ppermute | solution.py:280
  131.6 10.5 %collective-permute-start.36 = (bf16[256,256]{1,0:T(8,128)(2,1)S(1)}, bf16[256,256]{1,0:T(8,128)(2,1)S(1)}, u32[]{:S(2)}, u32[]{:S(2)}) collective-permute-start(bf16[256,256]{1,0:T(8,128)(2,1)S(1)} %get-tuple-element.57), channel_id=1, source_target_pairs={{0,8},{1,33},{2,10},{3,35},{4,12},{5,37},{6,14},{7,39},{8,16},{9,4... | collective-permute-start | bytes 393224 | tf_op jit(solution)/shard_map/ppermute | solution.py:280
  131.9 10.1 %collective-permute-start.37 = (bf16[256,256]{1,0:T(8,128)(2,1)S(1)}, bf16[256,256]{1,0:T(8,128)(2,1)S(1)}, u32[]{:S(2)}, u32[]{:S(2)}) collective-permute-start(bf16[256,256]{1,0:T(8,128)(2,1)S(1)} %get-tuple-element.58), channel_id=1, source_target_pairs={{0,16},{1,65},{2,18},{3,67},{4,20},{5,69},{6,22},{7,71},{8,24},{9,... | collective-permute-start | bytes 393224 | tf_op jit(solution)/shard_map/ppermute | solution.py:280
  149.5 9.6 %collective-permute-start.50 = (bf16[256,256]{1,0:T(8,128)(2,1)S(1)}, bf16[256,256]{1,0:T(8,128)(2,1)S(1)}, u32[]{:S(2)}, u32[]{:S(2)}) collective-permute-start(bf16[256,256]{1,0:T(8,128)(2,1)S(1)} %get-tuple-element.69.refs_0_.refs_1_), channel_id=1, source_target_pairs={{0,24},{1,97},{2,26},{3,99},{4,28},{5,101},{6,30},{7,103},{8,0},{9... | collective-permute-start | bytes 393224 | tf_op jit(solution)/shard_map/ppermute | solution.py:280
  154.0 18.5 %collective-permute-start.53 = (bf16[768,256]{1,0:T(8,128)(2,1)S(1)}, bf16[768,256]{1,0:T(8,128)(2,1)S(1)}, u32[]{:S(2)}, u32[]{:S(2)}) collective-permute-start(bf16[768,256]{1,0:T(8,128)(2,1)S(1)} %shard_map.151), channel_id=1, source_target_pairs={{0,24},{1,97},{2,26},{3,99},{4,28},{5,101},{6,30},{7,103},{8,0},{9... | collective-permute-start | bytes 1179656 | tf_op jit(solution)/shard_map/ppermute | solution.py:280
  155.3 17.2 %collective-permute-start.52 = (bf16[768,256]{1,0:T(8,128)(2,1)S(1)}, bf16[768,256]{1,0:T(8,128)(2,1)S(1)}, u32[]{:S(2)}, u32[]{:S(2)}) collective-permute-start(bf16[768,256]{1,0:T(8,128)(2,1)S(1)} %shard_map.151), channel_id=1, source_target_pairs={{0,16},{1,65},{2,18},{3,67},{4,20},{5,69},{6,22},{7,71},{8,24},{9,... | collective-permute-start | bytes 1179656 | tf_op jit(solution)/shard_map/ppermute | solution.py:280
  155.3 17.2 %collective-permute-start.51 = (bf16[768,256]{1,0:T(8,128)(2,1)S(1)}, bf16[768,256]{1,0:T(8,128)(2,1)S(1)}, u32[]{:S(2)}, u32[]{:S(2)}) collective-permute-start(bf16[768,256]{1,0:T(8,128)(2,1)S(1)} %shard_map.151), channel_id=1, source_target_pairs={{0,8},{1,33},{2,10},{3,35},{4,12},{5,37},{6,14},{7,39},{8,16},{9,4... | collective-permute-start | bytes 1179656 | tf_op jit(solution)/shard_map/ppermute | solution.py:280
  156.0 13.2 %collective-permute-start.49 = (bf16[256,256]{1,0:T(8,128)(2,1)S(1)}, bf16[256,256]{1,0:T(8,128)(2,1)S(1)}, u32[]{:S(2)}, u32[]{:S(2)}) collective-permute-start(bf16[256,256]{1,0:T(8,128)(2,1)S(1)} %get-tuple-element.69.refs_0_.refs_1_), channel_id=1, source_target_pairs={{0,16},{1,65},{2,18},{3,67},{4,20},{5,69},{6,22},{7,71},{8,24},{9,... | collective-permute-start | bytes 393224 | tf_op jit(solution)/shard_map/ppermute | solution.py:280
  159.2 11.3 %collective-permute-start.48 = (bf16[256,256]{1,0:T(8,128)(2,1)S(1)}, bf16[256,256]{1,0:T(8,128)(2,1)S(1)}, u32[]{:S(2)}, u32[]{:S(2)}) collective-permute-start(bf16[256,256]{1,0:T(8,128)(2,1)S(1)} %get-tuple-element.69.refs_0_.refs_1_), channel_id=1, source_target_pairs={{0,8},{1,33},{2,10},{3,35},{4,12},{5,37},{6,14},{7,39},{8,16},{9,4... | collective-permute-start | bytes 393224 | tf_op jit(solution)/shard_map/ppermute | solution.py:280
  180.3 8.8 %collective-permute-start.55 = (bf16[256,256]{1,0:T(8,128)(2,1)S(1)}, bf16[256,256]{1,0:T(8,128)(2,1)S(1)}, u32[]{:S(2)}, u32[]{:S(2)}) collective-permute-start(bf16[256,256]{1,0:T(8,128)(2,1)S(1)} %get-tuple-element.71), channel_id=1, source_target_pairs={{0,2},{1,3},{2,4},{3,5},{4,6},{5,7},{6,0},{7,1},{8,10},{9,11},{10,... | collective-permute-start | bytes 393224 | tf_op jit(solution)/shard_map/ppermute | solution.py:280
  (38 other events, 284.8 us)

commit v2 on v1

--- a/solution.py
+++ b/solution.py
@@ -202,9 +202,9 @@
         block = own[a * T : (a + 1) * T, :]
         for rest in rests:
             block = block + rest[a * T : (a + 1) * T, :].astype(f32)
-        out[:T, :] = block
+        out[:T, :] = block.astype(out.dtype)
         if extra:
-            out[T:, :] = one_row(total)
+            out[T:, :] = three_parts(total) if out.dtype == bf16 else one_row(total)
 
 
 def join_kernel(extra, mine, other, *outs):
@@ -357,10 +357,8 @@
         rests = sent([rests[k] for k in range(1, N4)], to_big)
         own, own_rest, moved, firsts = backward_near(matrix, pieces, extra)
         firsts = sent(firsts, to_big)
-        tall = WIDE if extra else T
-        *blocks, moved = call(
-            lambda *refs: big_sum_kernel(extra, *refs), [((tall, T), f32)] * 3 + [line], own_rest, moved, *rests,
-        )
+        block = ((WIDE, T), f32) if extra else ((T, T), bf16)
+        *blocks, moved = call(lambda *refs: big_sum_kernel(extra, *refs), [block] * 3 + [line], own_rest, moved, *rests)
         return [own, *firsts, *sent(blocks, to_small)], moved
 
     def to_rows(ahead, extra):

time: 191 us -> 186 us (0.974)
  waiting for transfers between devices: 76.4 us -> 73.1 us
    ppermute x58, waiting for transfers between devices: 76.4 us -> 73.1 us  [permute(): return lax.ppermute(value, ROW_COL, [(flat(p), flat(q)) for p, q in places])]
  transfers between devices with their start and end apart: 58 -> 58, of which waited for: 29 -> 31; matrix products, arithmetic and copies ran while one was open for 0% -> 0% of each run, Pallas kernels for 10% -> 10%
where the time goes in v2:
time: 186 us
  starting transfers between devices  77.9 us (42%)
  waiting for transfers between devices  73.1 us (39%)
  Pallas kernels  26.2 us (14%)
  local copies, waits for them, and re-layouts  6.88 us (4%)
    ppermute x58, starting transfers between devices, permute(): return lax.ppermute(value, ROW_COL, [(flat(p), flat(q)) for p, q in places])  77.9 us
    ppermute x58, waiting for transfers between devices, permute(): return lax.ppermute(value, ROW_COL, [(flat(p), flat(q)) for p, q in places])  73.1 us
    pallas_call x14, Pallas kernels, multiply(): pl.pallas_call(kernel, out_shape=[jax.ShapeDtypeStruct(*out) for out in o...  19.9 us
    unnamed x24, local copies, waits for them, and re-layouts  6.88 us
  transfers between devices with their start and end apart: 58, of which 31 were waited for; matrix products, arithmetic and copies ran while one was open for 0% of the time, Pallas kernels for 10%

profile of v2, /device:TPU:1, one launch (start us, length us, event | category | flops | bytes accessed | tf_op | source)
XLA Modules:
  0.0 185.7 jit_solution(13696504145588069428)
XLA Ops:
  1.7 3.4 %collective-permute-start.2 = (bf16[256,256]{1,0:T(8,128)(2,1)S(1)}, bf16[256,256]{1,0:T(8,128)(2,1)S(1)}, u32[]{:S(2)}, u32[]{:S(2)}) collective-permute-start(bf16[256,256]{1,0:T(8,128)(2,1)S(1)} %shard_map.131.refs_0_), channel_id=1, source_target_pairs={{0,6},{1,7},{2,0},{3,1},{4,2},{5,3},{6,4},{7,5},{8,14},{9,15},{10,... | collective-permute-start | bytes 393224 | tf_op jit(solution)/shard_map/ppermute | solution.py:280
  6.8 4.6 %copy-done = bf16[1,1,96,256,256]{4,3,2,1,0:T(8,128)(2,1)S(1)} copy-done((bf16[1,1,96,256,256]{4,3,2,1,0:T(8,128)(2,1)S(1)}, bf16[1,1,96,256,256]{4,3,2,1,0:T(8,128)(2,1)}, u32[]{:S(2)}) %copy-start) | copy-done | bytes 12582936
  12.7 2.9 %dense.1 = bf16[128,256,256]{2,1,0:T(8,128)(2,1)S(1)} custom-call(s32[1,1,96]{2,1,0:T(1,128)S(1)} %copy-done.10, s32[1,1,96]{2,1,0:T(1,128)S(1)} %copy-done.11, s32[1,1]{1,0:T(1,128)S(6)} %copy.14.count, bf16[1,1,96,256,256]{4,3,2,1,0:T(8,128)(2,1)S(1)} %copy-done), custom_call_target="tpu_custom_call" | custom-call | tf_op jit(solution)/shard_map/dense/pallas_call | solution.py:85
  22.4 2.7 %collective-permute-start.11 = (bf16[768,256]{1,0:T(8,128)(2,1)S(1)}, bf16[768,256]{1,0:T(8,128)(2,1)S(1)}, u32[]{:S(2)}, u32[]{:S(2)}) collective-permute-start(bf16[768,256]{1,0:T(8,128)(2,1)S(1)} %shard_map.134), channel_id=1, source_target_pairs={{0,16},{1,65},{2,18},{3,67},{4,20},{5,69},{6,22},{7,71},{8,24},{9,... | collective-permute-start | bytes 1179656 | tf_op jit(solution)/shard_map/ppermute | solution.py:280
  27.3 2.1 %shard_map.132 = (f32[256,256]{1,0:T(8,128)S(1)}, f32[768,256]{1,0:T(8,128)S(1)}, f32[1,256]{1,0:T(1,128)S(1)}, bf16[256,256]{1,0:T(8,128)(2,1)S(1)}, bf16[256,2...) custom-call(bf16[128,256,256]{2,1,0:T(8,128)(2,1)S(1)} %dense.1, bf16[256,256]{1,0:T(8,128)(2,1)S(1)} %shard_map.131.refs_0_, ...), custom_call_target="tpu_custom_call" | custom-call | flops 1879048192 | bytes 7340032 | tf_op jit(solution)/shard_map/pallas_call | solution.py:107
  36.5 3.3 %collective-permute-start.14 = (bf16[256,256]{1,0:T(8,128)(2,1)S(1)}, bf16[256,256]{1,0:T(8,128)(2,1)S(1)}, u32[]{:S(2)}, u32[]{:S(2)}) collective-permute-start(bf16[256,256]{1,0:T(8,128)(2,1)S(1)} %get-tuple-element.48), channel_id=1, source_target_pairs={{0,64},{1,17},{2,66},{3,19},{4,68},{5,21},{6,70},{7,23},{8,72},{9,... | collective-permute-start | bytes 393224 | tf_op jit(solution)/shard_map/ppermute | solution.py:280
  41.0 2.6 %collective-permute-done.14.refs_5_ = bf16[256,256]{1,0:T(8,128)(2,1)S(1)} collective-permute-done((bf16[256,256]{1,0:T(8,128)(2,1)S(1)}, bf16[256,256]{1,0:T(8,128)(2,1)S(1)}, u32[]{:S(2)}, u32[]{:S(2)}) %collective-permute-start.14) | collective-permute-done | bytes 131104 | tf_op jit(solution)/shard_map/ppermute | solution.py:280
  43.9 2.0 %collective-permute-start.18 = (bf16[272,256]{1,0:T(8,128)(2,1)S(1)}, bf16[272,256]{1,0:T(8,128)(2,1)S(1)}, u32[]{:S(2)}, u32[]{:S(2)}) collective-permute-start(bf16[272,256]{1,0:T(8,128)(2,1)S(1)} %get-tuple-element.50.refs_0_.refs_1_), channel_id=1, source_target_pairs={{0,96},{1,25},{2,98},{3,27},{4,100},{5,29},{6,102},{7,31},{8,104},... | collective-permute-start | bytes 417800 | tf_op jit(solution)/shard_map/ppermute | solution.py:280
  46.8 2.4 %collective-permute-start.21 = (bf16[272,256]{1,0:T(8,128)(2,1)S(1)}, bf16[272,256]{1,0:T(8,128)(2,1)S(1)}, u32[]{:S(2)}, u32[]{:S(2)}) collective-permute-start(bf16[272,256]{1,0:T(8,128)(2,1)S(1)} %get-tuple-element.50.refs_0_.refs_1_), channel_id=1, source_target_pairs={{0,24},{1,97},{2,26},{3,99},{4,28},{5,101},{6,30},{7,103},{8,0},{9... | collective-permute-start | bytes 417800 | tf_op jit(solution)/shard_map/ppermute | solution.py:280
  49.4 2.0 %collective-permute-done.17.refs_2_.refs_3_ = bf16[272,256]{1,0:T(8,128)(2,1)S(1)} collective-permute-done((bf16[272,256]{1,0:T(8,128)(2,1)S(1)}, bf16[272,256]{1,0:T(8,128)(2,1)S(1)}, u32[]{:S(2)}, u32[]{:S(2)}) %collective-permute-start.17) | collective-permute-done | bytes 139296 | tf_op jit(solution)/shard_map/ppermute | solution.py:280
  52.8 2.8 %collective-permute-start.24 = (bf16[784,256]{1,0:T(8,128)(2,1)S(1)}, bf16[784,256]{1,0:T(8,128)(2,1)S(1)}, u32[]{:S(2)}, u32[]{:S(2)}) collective-permute-start(bf16[784,256]{1,0:T(8,128)(2,1)S(1)} %shard_map.139), channel_id=1, source_target_pairs={{0,24},{1,97},{2,26},{3,99},{4,28},{5,101},{6,30},{7,103},{8,0},{9... | collective-permute-start | bytes 1204232 | tf_op jit(solution)/shard_map/ppermute | solution.py:280
  60.5 9.4 %collective-permute-done.20.refs_5_ = bf16[272,256]{1,0:T(8,128)(2,1)S(1)} collective-permute-done((bf16[272,256]{1,0:T(8,128)(2,1)S(1)}, bf16[272,256]{1,0:T(8,128)(2,1)S(1)}, u32[]{:S(2)}, u32[]{:S(2)}) %collective-permute-start.20) | collective-permute-done | bytes 139296 | tf_op jit(solution)/shard_map/ppermute | solution.py:280
  71.5 2.1 %shard_map.138.refs_0_ = f32[8,256,256]{2,1,0:T(8,128)S(1)} custom-call(bf16[128,256,256]{2,1,0:T(8,128)(2,1)S(1)} %dense.1, bf16[272,256]{1,0:T(8,128)(2,1)S(1)} %get-tuple-element.50.refs_0_.refs_1_, bf16[272,256]{1,0:T(8,128)(2,1)S(1)} %collective-permute-done.16.refs_1_.refs_2_, bf16[272,256]{1,0:T(8,128)(2,1)S(1)} %collective-permute-done.17.refs_2_.refs_3_, ...), custom_call_target="tpu_custom_call" | custom-call | flops 1879048192 | bytes 7340032 | tf_op jit(solution)/shard_map/pallas_call | solution.py:107
  75.0 5.4 %collective-permute-start.25 = (f32[4,264,256]{2,1,0:T(8,128)S(1)}, f32[4,264,256]{2,1,0:T(8,128)S(1)}, u32[]{:S(2)}, u32[]{:S(2)}) collective-permute-start(f32[4,264,256]{2,1,0:T(8,128)S(1)} %shard_map.141), channel_id=1, source_target_pairs={{0,1},{1,0},{2,3},{3,2},{4,5},{5,4},{6,7},{7,6},{8,9},{9,8},{10,11... | collective-permute-start | bytes 3244040 | tf_op jit(solution)/shard_map/ppermute | solution.py:280
  86.9 2.1 %collective-permute-done.26.refs_1_ = bf16[272,256]{1,0:T(8,128)(2,1)S(1)} collective-permute-done((bf16[272,256]{1,0:T(8,128)(2,1)S(1)}, bf16[272,256]{1,0:T(8,128)(2,1)S(1)}, u32[]{:S(2)}, u32[]{:S(2)}) %collective-permute-start.26) | collective-permute-done | bytes 139296 | tf_op jit(solution)/shard_map/ppermute | solution.py:280
  89.0 3.6 %collective-permute-done.27.refs_2_ = bf16[272,256]{1,0:T(8,128)(2,1)S(1)} collective-permute-done((bf16[272,256]{1,0:T(8,128)(2,1)S(1)}, bf16[272,256]{1,0:T(8,128)(2,1)S(1)}, u32[]{:S(2)}, u32[]{:S(2)}) %collective-permute-start.27) | collective-permute-done | bytes 139296 | tf_op jit(solution)/shard_map/ppermute | solution.py:280
  92.7 3.1 %collective-permute-start.31 = (bf16[272,256]{1,0:T(8,128)(2,1)S(1)}, bf16[272,256]{1,0:T(8,128)(2,1)S(1)}, u32[]{:S(2)}, u32[]{:S(2)}) collective-permute-start(bf16[272,256]{1,0:T(8,128)(2,1)S(1)} %get-tuple-element.55.refs_0_), channel_id=1, source_target_pairs={{0,6},{1,7},{2,0},{3,1},{4,2},{5,3},{6,4},{7,5},{8,14},{9,15},{10,... | collective-permute-start | bytes 417800 | tf_op jit(solution)/shard_map/ppermute | solution.py:280
  97.7 3.7 %collective-permute-done.31.refs_3_ = bf16[272,256]{1,0:T(8,128)(2,1)S(1)} collective-permute-done((bf16[272,256]{1,0:T(8,128)(2,1)S(1)}, bf16[272,256]{1,0:T(8,128)(2,1)S(1)}, u32[]{:S(2)}, u32[]{:S(2)}) %collective-permute-start.31) | collective-permute-done | bytes 139296 | tf_op jit(solution)/shard_map/ppermute | solution.py:280
  102.8 2.0 %collective-permute-start.34 = (bf16[272,256]{1,0:T(8,128)(2,1)S(1)}, bf16[272,256]{1,0:T(8,128)(2,1)S(1)}, u32[]{:S(2)}, u32[]{:S(2)}) collective-permute-start(bf16[272,256]{1,0:T(8,128)(2,1)S(1)} %collective-permute-done.30.refs_2_), channel_id=1, source_target_pairs={{0,1},{1,0},{2,3},{3,2},{4,5},{5,4},{6,7},{7,6},{8,9},{9,8},{10,11... | collective-permute-start | bytes 417800 | tf_op jit(solution)/shard_map/ppermute | solution.py:280
  109.6 2.1 %collective-permute-start.40 = (bf16[784,256]{1,0:T(8,128)(2,1)S(1)}, bf16[784,256]{1,0:T(8,128)(2,1)S(1)}, u32[]{:S(2)}, u32[]{:S(2)}) collective-permute-start(bf16[784,256]{1,0:T(8,128)(2,1)S(1)} %shard_map.146), channel_id=1, source_target_pairs={{0,16},{1,65},{2,18},{3,67},{4,20},{5,69},{6,22},{7,71},{8,24},{9,... | collective-permute-start | bytes 1204232 | tf_op jit(solution)/shard_map/ppermute | solution.py:280
  113.4 2.1 %shard_map.144 = (f32[256,256]{1,0:T(8,128)S(1)}, f32[768,256]{1,0:T(8,128)S(1)}, f32[1,256]{1,0:T(1,128)S(1)}, bf16[256,256]{1,0:T(8,128)(2,1)S(1)}, bf16[256,2...) custom-call(bf16[128,256,256]{2,1,0:T(8,128)(2,1)S(1)} %dense.1, bf16[272,256]{1,0:T(8,128)(2,1)S(1)} %get-tuple-element.55.refs_0_, ...), custom_call_target="tpu_custom_call" | custom-call | flops 1879048192 | bytes 7340032 | tf_op jit(solution)/shard_map/pallas_call | solution.py:107
  115.5 5.6 %collective-permute-done.39.refs_2_ = bf16[784,256]{1,0:T(8,128)(2,1)S(1)} collective-permute-done((bf16[784,256]{1,0:T(8,128)(2,1)S(1)}, bf16[784,256]{1,0:T(8,128)(2,1)S(1)}, u32[]{:S(2)}, u32[]{:S(2)}) %collective-permute-start.39) | collective-permute-done | bytes 401440 | tf_op jit(solution)/shard_map/ppermute | solution.py:280
  125.1 2.0 %collective-permute-start.44 = (f32[264,256]{1,0:T(8,128)S(1)}, f32[264,256]{1,0:T(8,128)S(1)}, u32[]{:S(2)}, u32[]{:S(2)}) collective-permute-start(f32[264,256]{1,0:T(8,128)S(1)} %get-tuple-element.64), channel_id=1, source_target_pairs={{0,96},{1,25},{2,98},{3,27},{4,100},{5,29},{6,102},{7,31},{8,104},... | collective-permute-start | bytes 811016 | tf_op jit(solution)/shard_map/ppermute | solution.py:280
  127.0 3.2 %collective-permute-start.37 = (bf16[256,256]{1,0:T(8,128)(2,1)S(1)}, bf16[256,256]{1,0:T(8,128)(2,1)S(1)}, u32[]{:S(2)}, u32[]{:S(2)}) collective-permute-start(bf16[256,256]{1,0:T(8,128)(2,1)S(1)} %get-tuple-element.58), channel_id=1, source_target_pairs={{0,16},{1,65},{2,18},{3,67},{4,20},{5,69},{6,22},{7,71},{8,24},{9,... | collective-permute-start | bytes 393224 | tf_op jit(solution)/shard_map/ppermute | solution.py:280
  130.3 7.2 %collective-permute-done.36.refs_1_ = bf16[256,256]{1,0:T(8,128)(2,1)S(1)} collective-permute-done((bf16[256,256]{1,0:T(8,128)(2,1)S(1)}, bf16[256,256]{1,0:T(8,128)(2,1)S(1)}, u32[]{:S(2)}, u32[]{:S(2)}) %collective-permute-start.36) | collective-permute-done | bytes 131104 | tf_op jit(solution)/shard_map/ppermute | solution.py:280
  137.4 3.8 %collective-permute-done.38.refs_3_ = bf16[256,256]{1,0:T(8,128)(2,1)S(1)} collective-permute-done((bf16[256,256]{1,0:T(8,128)(2,1)S(1)}, bf16[256,256]{1,0:T(8,128)(2,1)S(1)}, u32[]{:S(2)}, u32[]{:S(2)}) %collective-permute-start.38) | collective-permute-done | bytes 131104 | tf_op jit(solution)/shard_map/ppermute | solution.py:280
  147.5 1.9 %collective-permute-done.45.refs_1_.refs_2_ = bf16[256,256]{1,0:T(8,128)(2,1)S(1)} collective-permute-done((bf16[256,256]{1,0:T(8,128)(2,1)S(1)}, bf16[256,256]{1,0:T(8,128)(2,1)S(1)}, u32[]{:S(2)}, u32[]{:S(2)}) %collective-permute-start.45) | collective-permute-done | bytes 131104 | tf_op jit(solution)/shard_map/ppermute | solution.py:280
  151.4 3.2 %collective-permute-start.49 = (bf16[256,256]{1,0:T(8,128)(2,1)S(1)}, bf16[256,256]{1,0:T(8,128)(2,1)S(1)}, u32[]{:S(2)}, u32[]{:S(2)}) collective-permute-start(bf16[256,256]{1,0:T(8,128)(2,1)S(1)} %get-tuple-element.69.refs_0_.refs_1_), channel_id=1, source_target_pairs={{0,16},{1,65},{2,18},{3,67},{4,20},{5,69},{6,22},{7,71},{8,24},{9,... | collective-permute-start | bytes 393224 | tf_op jit(solution)/shard_map/ppermute | solution.py:280
  154.6 10.1 %collective-permute-done.49.refs_5_ = bf16[256,256]{1,0:T(8,128)(2,1)S(1)} collective-permute-done((bf16[256,256]{1,0:T(8,128)(2,1)S(1)}, bf16[256,256]{1,0:T(8,128)(2,1)S(1)}, u32[]{:S(2)}, u32[]{:S(2)}) %collective-permute-start.49) | collective-permute-done | bytes 131104 | tf_op jit(solution)/shard_map/ppermute | solution.py:280
  165.9 2.1 %shard_map.150.refs_0_ = f32[8,256,256]{2,1,0:T(8,128)S(1)} custom-call(bf16[128,256,256]{2,1,0:T(8,128)(2,1)S(1)} %dense.1, bf16[256,256]{1,0:T(8,128)(2,1)S(1)} %get-tuple-element.69.refs_0_.refs_1_, bf16[256,256]{1,0:T(8,128)(2,1)S(1)} %collective-permute-done.45.refs_1_.refs_2_, bf16[256,256]{1,0:T(8,128)(2,1)S(1)} %collective-permute-done.46.refs_2_.refs_3_, ...), custom_call_target="tpu_custom_call" | custom-call | flops 1879048192 | bytes 7340032 | tf_op jit(solution)/shard_map/pallas_call | solution.py:107
  169.4 3.9 %collective-permute-start.54 = (f32[4,256,256]{2,1,0:T(8,128)S(1)}, f32[4,256,256]{2,1,0:T(8,128)S(1)}, u32[]{:S(2)}, u32[]{:S(2)}) collective-permute-start(f32[4,256,256]{2,1,0:T(8,128)S(1)} %shard_map.153), channel_id=1, source_target_pairs={{0,1},{1,0},{2,3},{3,2},{4,5},{5,4},{6,7},{7,6},{8,9},{9,8},{10,11... | collective-permute-start | bytes 3145736 | tf_op jit(solution)/shard_map/ppermute | solution.py:280
  178.6 5.9 %collective-permute-done.55.refs_1_ = bf16[256,256]{1,0:T(8,128)(2,1)S(1)} collective-permute-done((bf16[256,256]{1,0:T(8,128)(2,1)S(1)}, bf16[256,256]{1,0:T(8,128)(2,1)S(1)}, u32[]{:S(2)}, u32[]{:S(2)}) %collective-permute-start.55) | collective-permute-done | bytes 131104 | tf_op jit(solution)/shard_map/ppermute | solution.py:280
  (134 shorter events, 69.2 us)
Async XLA Ops:
  1.7 15.5 %collective-permute-start.2 = (bf16[256,256]{1,0:T(8,128)(2,1)S(1)}, bf16[256,256]{1,0:T(8,128)(2,1)S(1)}, u32[]{:S(2)}, u32[]{:S(2)}) collective-permute-start(bf16[256,256]{1,0:T(8,128)(2,1)S(1)} %shard_map.131.refs_0_), channel_id=1, source_target_pairs={{0,6},{1,7},{2,0},{3,1},{4,2},{5,3},{6,4},{7,5},{8,14},{9,15},{10,... | collective-permute-start | bytes 393224 | tf_op jit(solution)/shard_map/ppermute | solution.py:280
  5.1 12.2 %collective-permute-start.1 = (bf16[256,256]{1,0:T(8,128)(2,1)S(1)}, bf16[256,256]{1,0:T(8,128)(2,1)S(1)}, u32[]{:S(2)}, u32[]{:S(2)}) collective-permute-start(bf16[256,256]{1,0:T(8,128)(2,1)S(1)} %shard_map.131.refs_0_), channel_id=1, source_target_pairs={{0,4},{1,5},{2,6},{3,7},{4,0},{5,1},{6,2},{7,3},{8,12},{9,13},{10,... | collective-permute-start | bytes 393224 | tf_op jit(solution)/shard_map/ppermute | solution.py:280
  5.6 12.1 %collective-permute-start = (bf16[256,256]{1,0:T(8,128)(2,1)S(1)}, bf16[256,256]{1,0:T(8,128)(2,1)S(1)}, u32[]{:S(2)}, u32[]{:S(2)}) collective-permute-start(bf16[256,256]{1,0:T(8,128)(2,1)S(1)} %shard_map.131.refs_0_), channel_id=1, source_target_pairs={{0,2},{1,3},{2,4},{3,5},{4,6},{5,7},{6,0},{7,1},{8,10},{9,11},{10,... | collective-permute-start | bytes 393224 | tf_op jit(solution)/shard_map/ppermute | solution.py:280
  20.1 10.6 %collective-permute-start.10 = (bf16[768,256]{1,0:T(8,128)(2,1)S(1)}, bf16[768,256]{1,0:T(8,128)(2,1)S(1)}, u32[]{:S(2)}, u32[]{:S(2)}) collective-permute-start(bf16[768,256]{1,0:T(8,128)(2,1)S(1)} %shard_map.133), channel_id=1, source_target_pairs={{0,8},{1,33},{2,10},{3,35},{4,12},{5,37},{6,14},{7,39},{8,16},{9,4... | collective-permute-start | bytes 1179656 | tf_op jit(solution)/shard_map/ppermute | solution.py:280
  22.4 11.3 %collective-permute-start.11 = (bf16[768,256]{1,0:T(8,128)(2,1)S(1)}, bf16[768,256]{1,0:T(8,128)(2,1)S(1)}, u32[]{:S(2)}, u32[]{:S(2)}) collective-permute-start(bf16[768,256]{1,0:T(8,128)(2,1)S(1)} %shard_map.134), channel_id=1, source_target_pairs={{0,16},{1,65},{2,18},{3,67},{4,20},{5,69},{6,22},{7,71},{8,24},{9,... | collective-permute-start | bytes 1179656 | tf_op jit(solution)/shard_map/ppermute | solution.py:280
  29.4 10.4 %collective-permute-start.7 = (bf16[256,256]{1,0:T(8,128)(2,1)S(1)}, bf16[256,256]{1,0:T(8,128)(2,1)S(1)}, u32[]{:S(2)}, u32[]{:S(2)}) collective-permute-start(bf16[256,256]{1,0:T(8,128)(2,1)S(1)} %get-tuple-element.42), channel_id=1, source_target_pairs={{0,8},{1,33},{2,10},{3,35},{4,12},{5,37},{6,14},{7,39},{8,16},{9,4... | collective-permute-start | bytes 393224 | tf_op jit(solution)/shard_map/ppermute | solution.py:280
  29.9 10.6 %collective-permute-start.8 = (bf16[256,256]{1,0:T(8,128)(2,1)S(1)}, bf16[256,256]{1,0:T(8,128)(2,1)S(1)}, u32[]{:S(2)}, u32[]{:S(2)}) collective-permute-start(bf16[256,256]{1,0:T(8,128)(2,1)S(1)} %get-tuple-element.43), channel_id=1, source_target_pairs={{0,16},{1,65},{2,18},{3,67},{4,20},{5,69},{6,22},{7,71},{8,24},{9,... | collective-permute-start | bytes 393224 | tf_op jit(solution)/shard_map/ppermute | solution.py:280
  30.7 9.8 %collective-permute-start.9 = (bf16[256,256]{1,0:T(8,128)(2,1)S(1)}, bf16[256,256]{1,0:T(8,128)(2,1)S(1)}, u32[]{:S(2)}, u32[]{:S(2)}) collective-permute-start(bf16[256,256]{1,0:T(8,128)(2,1)S(1)} %get-tuple-element.44), channel_id=1, source_target_pairs={{0,24},{1,97},{2,26},{3,99},{4,28},{5,101},{6,30},{7,103},{8,0},{9... | collective-permute-start | bytes 393224 | tf_op jit(solution)/shard_map/ppermute | solution.py:280
  46.8 12.3 %collective-permute-start.21 = (bf16[272,256]{1,0:T(8,128)(2,1)S(1)}, bf16[272,256]{1,0:T(8,128)(2,1)S(1)}, u32[]{:S(2)}, u32[]{:S(2)}) collective-permute-start(bf16[272,256]{1,0:T(8,128)(2,1)S(1)} %get-tuple-element.50.refs_0_.refs_1_), channel_id=1, source_target_pairs={{0,24},{1,97},{2,26},{3,99},{4,28},{5,101},{6,30},{7,103},{8,0},{9... | collective-permute-start | bytes 417800 | tf_op jit(solution)/shard_map/ppermute | solution.py:280
  52.8 20.7 %collective-permute-start.24 = (bf16[784,256]{1,0:T(8,128)(2,1)S(1)}, bf16[784,256]{1,0:T(8,128)(2,1)S(1)}, u32[]{:S(2)}, u32[]{:S(2)}) collective-permute-start(bf16[784,256]{1,0:T(8,128)(2,1)S(1)} %shard_map.139), channel_id=1, source_target_pairs={{0,24},{1,97},{2,26},{3,99},{4,28},{5,101},{6,30},{7,103},{8,0},{9... | collective-permute-start | bytes 1204232 | tf_op jit(solution)/shard_map/ppermute | solution.py:280
  55.7 17.9 %collective-permute-start.23 = (bf16[784,256]{1,0:T(8,128)(2,1)S(1)}, bf16[784,256]{1,0:T(8,128)(2,1)S(1)}, u32[]{:S(2)}, u32[]{:S(2)}) collective-permute-start(bf16[784,256]{1,0:T(8,128)(2,1)S(1)} %shard_map.139), channel_id=1, source_target_pairs={{0,16},{1,65},{2,18},{3,67},{4,20},{5,69},{6,22},{7,71},{8,24},{9,... | collective-permute-start | bytes 1204232 | tf_op jit(solution)/shard_map/ppermute | solution.py:280
  57.2 16.3 %collective-permute-start.22 = (bf16[784,256]{1,0:T(8,128)(2,1)S(1)}, bf16[784,256]{1,0:T(8,128)(2,1)S(1)}, u32[]{:S(2)}, u32[]{:S(2)}) collective-permute-start(bf16[784,256]{1,0:T(8,128)(2,1)S(1)} %shard_map.139), channel_id=1, source_target_pairs={{0,8},{1,33},{2,10},{3,35},{4,12},{5,37},{6,14},{7,39},{8,16},{9,4... | collective-permute-start | bytes 1204232 | tf_op jit(solution)/shard_map/ppermute | solution.py:280
  57.2 12.6 %collective-permute-start.20 = (bf16[272,256]{1,0:T(8,128)(2,1)S(1)}, bf16[272,256]{1,0:T(8,128)(2,1)S(1)}, u32[]{:S(2)}, u32[]{:S(2)}) collective-permute-start(bf16[272,256]{1,0:T(8,128)(2,1)S(1)} %get-tuple-element.50.refs_0_.refs_1_), channel_id=1, source_target_pairs={{0,16},{1,65},{2,18},{3,67},{4,20},{5,69},{6,22},{7,71},{8,24},{9,... | collective-permute-start | bytes 417800 | tf_op jit(solution)/shard_map/ppermute | solution.py:280
  59.1 12.4 %collective-permute-start.19 = (bf16[272,256]{1,0:T(8,128)(2,1)S(1)}, bf16[272,256]{1,0:T(8,128)(2,1)S(1)}, u32[]{:S(2)}, u32[]{:S(2)}) collective-permute-start(bf16[272,256]{1,0:T(8,128)(2,1)S(1)} %get-tuple-element.50.refs_0_.refs_1_), channel_id=1, source_target_pairs={{0,8},{1,33},{2,10},{3,35},{4,12},{5,37},{6,14},{7,39},{8,16},{9,4... | collective-permute-start | bytes 417800 | tf_op jit(solution)/shard_map/ppermute | solution.py:280
  96.7 9.3 %collective-permute-start.29 = (bf16[272,256]{1,0:T(8,128)(2,1)S(1)}, bf16[272,256]{1,0:T(8,128)(2,1)S(1)}, u32[]{:S(2)}, u32[]{:S(2)}) collective-permute-start(bf16[272,256]{1,0:T(8,128)(2,1)S(1)} %get-tuple-element.55.refs_0_), channel_id=1, source_target_pairs={{0,2},{1,3},{2,4},{3,5},{4,6},{5,7},{6,0},{7,1},{8,10},{9,11},{10,... | collective-permute-start | bytes 417800 | tf_op jit(solution)/shard_map/ppermute | solution.py:280
  96.7 9.8 %collective-permute-start.32 = (bf16[272,256]{1,0:T(8,128)(2,1)S(1)}, bf16[272,256]{1,0:T(8,128)(2,1)S(1)}, u32[]{:S(2)}, u32[]{:S(2)}) collective-permute-start(bf16[272,256]{1,0:T(8,128)(2,1)S(1)} %get-tuple-element.55.refs_0_), channel_id=1, source_target_pairs={{0,1},{1,0},{2,3},{3,2},{4,5},{5,4},{6,7},{7,6},{8,9},{9,8},{10,11... | collective-permute-start | bytes 417800 | tf_op jit(solution)/shard_map/ppermute | solution.py:280
  108.5 12.6 %collective-permute-start.39 = (bf16[784,256]{1,0:T(8,128)(2,1)S(1)}, bf16[784,256]{1,0:T(8,128)(2,1)S(1)}, u32[]{:S(2)}, u32[]{:S(2)}) collective-permute-start(bf16[784,256]{1,0:T(8,128)(2,1)S(1)} %shard_map.145), channel_id=1, source_target_pairs={{0,8},{1,33},{2,10},{3,35},{4,12},{5,37},{6,14},{7,39},{8,16},{9,4... | collective-permute-start | bytes 1204232 | tf_op jit(solution)/shard_map/ppermute | solution.py:280
  109.6 11.5 %collective-permute-start.40 = (bf16[784,256]{1,0:T(8,128)(2,1)S(1)}, bf16[784,256]{1,0:T(8,128)(2,1)S(1)}, u32[]{:S(2)}, u32[]{:S(2)}) collective-permute-start(bf16[784,256]{1,0:T(8,128)(2,1)S(1)} %shard_map.146), channel_id=1, source_target_pairs={{0,16},{1,65},{2,18},{3,67},{4,20},{5,69},{6,22},{7,71},{8,24},{9,... | collective-permute-start | bytes 1204232 | tf_op jit(solution)/shard_map/ppermute | solution.py:280
  112.7 10.1 %collective-permute-start.41 = (bf16[784,256]{1,0:T(8,128)(2,1)S(1)}, bf16[784,256]{1,0:T(8,128)(2,1)S(1)}, u32[]{:S(2)}, u32[]{:S(2)}) collective-permute-start(bf16[784,256]{1,0:T(8,128)(2,1)S(1)} %shard_map.147), channel_id=1, source_target_pairs={{0,24},{1,97},{2,26},{3,99},{4,28},{5,101},{6,30},{7,103},{8,0},{9... | collective-permute-start | bytes 1204232 | tf_op jit(solution)/shard_map/ppermute | solution.py:280
  123.0 18.3 %collective-permute-start.42 = (f32[264,256]{1,0:T(8,128)S(1)}, f32[264,256]{1,0:T(8,128)S(1)}, u32[]{:S(2)}, u32[]{:S(2)}) collective-permute-start(f32[264,256]{1,0:T(8,128)S(1)} %get-tuple-element.62), channel_id=1, source_target_pairs={{0,32},{1,9},{2,34},{3,11},{4,36},{5,13},{6,38},{7,15},{8,40},{9,1... | collective-permute-start | bytes 811016 | tf_op jit(solution)/shard_map/ppermute | solution.py:280
  123.5 17.7 %collective-permute-start.43 = (f32[264,256]{1,0:T(8,128)S(1)}, f32[264,256]{1,0:T(8,128)S(1)}, u32[]{:S(2)}, u32[]{:S(2)}) collective-permute-start(f32[264,256]{1,0:T(8,128)S(1)} %get-tuple-element.63), channel_id=1, source_target_pairs={{0,64},{1,17},{2,66},{3,19},{4,68},{5,21},{6,70},{7,23},{8,72},{9,... | collective-permute-start | bytes 811016 | tf_op jit(solution)/shard_map/ppermute | solution.py:280
  125.1 16.2 %collective-permute-start.44 = (f32[264,256]{1,0:T(8,128)S(1)}, f32[264,256]{1,0:T(8,128)S(1)}, u32[]{:S(2)}, u32[]{:S(2)}) collective-permute-start(f32[264,256]{1,0:T(8,128)S(1)} %get-tuple-element.64), channel_id=1, source_target_pairs={{0,96},{1,25},{2,98},{3,27},{4,100},{5,29},{6,102},{7,31},{8,104},... | collective-permute-start | bytes 811016 | tf_op jit(solution)/shard_map/ppermute | solution.py:280
  127.0 10.4 %collective-permute-start.36 = (bf16[256,256]{1,0:T(8,128)(2,1)S(1)}, bf16[256,256]{1,0:T(8,128)(2,1)S(1)}, u32[]{:S(2)}, u32[]{:S(2)}) collective-permute-start(bf16[256,256]{1,0:T(8,128)(2,1)S(1)} %get-tuple-element.57), channel_id=1, source_target_pairs={{0,8},{1,33},{2,10},{3,35},{4,12},{5,37},{6,14},{7,39},{8,16},{9,4... | collective-permute-start | bytes 393224 | tf_op jit(solution)/shard_map/ppermute | solution.py:280
  127.0 10.4 %collective-permute-start.37 = (bf16[256,256]{1,0:T(8,128)(2,1)S(1)}, bf16[256,256]{1,0:T(8,128)(2,1)S(1)}, u32[]{:S(2)}, u32[]{:S(2)}) collective-permute-start(bf16[256,256]{1,0:T(8,128)(2,1)S(1)} %get-tuple-element.58), channel_id=1, source_target_pairs={{0,16},{1,65},{2,18},{3,67},{4,20},{5,69},{6,22},{7,71},{8,24},{9,... | collective-permute-start | bytes 393224 | tf_op jit(solution)/shard_map/ppermute | solution.py:280
  145.0 9.6 %collective-permute-start.50 = (bf16[256,256]{1,0:T(8,128)(2,1)S(1)}, bf16[256,256]{1,0:T(8,128)(2,1)S(1)}, u32[]{:S(2)}, u32[]{:S(2)}) collective-permute-start(bf16[256,256]{1,0:T(8,128)(2,1)S(1)} %get-tuple-element.69.refs_0_.refs_1_), channel_id=1, source_target_pairs={{0,24},{1,97},{2,26},{3,99},{4,28},{5,101},{6,30},{7,103},{8,0},{9... | collective-permute-start | bytes 393224 | tf_op jit(solution)/shard_map/ppermute | solution.py:280
  149.5 18.5 %collective-permute-start.53 = (bf16[768,256]{1,0:T(8,128)(2,1)S(1)}, bf16[768,256]{1,0:T(8,128)(2,1)S(1)}, u32[]{:S(2)}, u32[]{:S(2)}) collective-permute-start(bf16[768,256]{1,0:T(8,128)(2,1)S(1)} %shard_map.151), channel_id=1, source_target_pairs={{0,24},{1,97},{2,26},{3,99},{4,28},{5,101},{6,30},{7,103},{8,0},{9... | collective-permute-start | bytes 1179656 | tf_op jit(solution)/shard_map/ppermute | solution.py:280
  150.7 17.2 %collective-permute-start.52 = (bf16[768,256]{1,0:T(8,128)(2,1)S(1)}, bf16[768,256]{1,0:T(8,128)(2,1)S(1)}, u32[]{:S(2)}, u32[]{:S(2)}) collective-permute-start(bf16[768,256]{1,0:T(8,128)(2,1)S(1)} %shard_map.151), channel_id=1, source_target_pairs={{0,16},{1,65},{2,18},{3,67},{4,20},{5,69},{6,22},{7,71},{8,24},{9,... | collective-permute-start | bytes 1179656 | tf_op jit(solution)/shard_map/ppermute | solution.py:280
  150.8 17.2 %collective-permute-start.51 = (bf16[768,256]{1,0:T(8,128)(2,1)S(1)}, bf16[768,256]{1,0:T(8,128)(2,1)S(1)}, u32[]{:S(2)}, u32[]{:S(2)}) collective-permute-start(bf16[768,256]{1,0:T(8,128)(2,1)S(1)} %shard_map.151), channel_id=1, source_target_pairs={{0,8},{1,33},{2,10},{3,35},{4,12},{5,37},{6,14},{7,39},{8,16},{9,4... | collective-permute-start | bytes 1179656 | tf_op jit(solution)/shard_map/ppermute | solution.py:280
  151.4 13.2 %collective-permute-start.49 = (bf16[256,256]{1,0:T(8,128)(2,1)S(1)}, bf16[256,256]{1,0:T(8,128)(2,1)S(1)}, u32[]{:S(2)}, u32[]{:S(2)}) collective-permute-start(bf16[256,256]{1,0:T(8,128)(2,1)S(1)} %get-tuple-element.69.refs_0_.refs_1_), channel_id=1, source_target_pairs={{0,16},{1,65},{2,18},{3,67},{4,20},{5,69},{6,22},{7,71},{8,24},{9,... | collective-permute-start | bytes 393224 | tf_op jit(solution)/shard_map/ppermute | solution.py:280
  154.6 11.3 %collective-permute-start.48 = (bf16[256,256]{1,0:T(8,128)(2,1)S(1)}, bf16[256,256]{1,0:T(8,128)(2,1)S(1)}, u32[]{:S(2)}, u32[]{:S(2)}) collective-permute-start(bf16[256,256]{1,0:T(8,128)(2,1)S(1)} %get-tuple-element.69.refs_0_.refs_1_), channel_id=1, source_target_pairs={{0,8},{1,33},{2,10},{3,35},{4,12},{5,37},{6,14},{7,39},{8,16},{9,4... | collective-permute-start | bytes 393224 | tf_op jit(solution)/shard_map/ppermute | solution.py:280
  175.8 8.8 %collective-permute-start.55 = (bf16[256,256]{1,0:T(8,128)(2,1)S(1)}, bf16[256,256]{1,0:T(8,128)(2,1)S(1)}, u32[]{:S(2)}, u32[]{:S(2)}) collective-permute-start(bf16[256,256]{1,0:T(8,128)(2,1)S(1)} %get-tuple-element.71), channel_id=1, source_target_pairs={{0,2},{1,3},{2,4},{3,5},{4,6},{5,7},{6,0},{7,1},{8,10},{9,11},{10,... | collective-permute-start | bytes 393224 | tf_op jit(solution)/shard_map/ppermute | solution.py:280
  175.8 8.7 %collective-permute-start.56 = (bf16[256,256]{1,0:T(8,128)(2,1)S(1)}, bf16[256,256]{1,0:T(8,128)(2,1)S(1)}, u32[]{:S(2)}, u32[]{:S(2)}) collective-permute-start(bf16[256,256]{1,0:T(8,128)(2,1)S(1)} %get-tuple-element.72), channel_id=1, source_target_pairs={{0,4},{1,5},{2,6},{3,7},{4,0},{5,1},{6,2},{7,3},{8,12},{9,13},{10,... | collective-permute-start | bytes 393224 | tf_op jit(solution)/shard_map/ppermute | solution.py:280
  (38 other events, 248.8 us)
